TPU v7x, 256 devices: a whole 4x4x8 slice. The times are simulated.
256 devices in a mesh: band: 32 (over z, x_hi, core), lane: 8 (over y, x_lo).
Axes of the slice: x: 4 (x_hi: 2, x_lo: 2; x = x_hi * 2 + x_lo), y: 4, z: 8, core: 2. Of those that a mesh axis runs over, the one named last changes fastest.
Arguments:
- load_terms: float32 [2048, 512, 256], P('band', 'lane'), may hold values from -6 to 6
- start_values: float32 [2048, 512, 256], P('band', 'lane'), may hold values from -6 to 6
- reaction_rate: float32 [2048, 512, 256], P('band', 'lane'), may hold values from 0.1 to 0.9
Outputs:
- solution: float32 [2048, 512, 256], P('band', 'lane')
- remaining: float32 [2048, 512, 256], P('band', 'lane')
All inputs are finite; a program needn't handle non-finite values.
Results may differ from a plain program's by a relative error of at most 0.0003.
Values sent between devices are 32-bit elements.
A program may use at most 128 MiB of HBM per device.

v0:
```python
import jax
import jax.numpy as jnp
from jax import lax
from jax.sharding import PartitionSpec as P

RATIO = 2
BEFORE = 3
AFTER = 2
INNER = 13


def extended(value, sides, width, wrap):
    edges = {}
    for axis, dim in sides:
        devices, length = lax.axis_size(axis), value.shape[dim]
        up = [(i, (i + 1) % devices) for i in range(devices if wrap else devices - 1)]
        last = lax.slice_in_dim(value, length - width, length, axis=dim)
        leading = lax.slice_in_dim(value, 0, width, axis=dim)
        edges[dim] = lax.ppermute(last, axis, up), lax.ppermute(
            leading, axis, [(b, a) for a, b in up]
        )
    done = []
    for _, dim in sides:
        low, high = edges[dim]
        around = [(width, width) if d in done else (0, 0) for d in range(value.ndim)]
        value = jnp.concatenate([jnp.pad(low, around), value, jnp.pad(high, around)], axis=dim)
        done.append(dim)
    return value


def padded_2(block, sides, width, periodic):
    for axis, dim in sides:
        count = lax.axis_size(axis)
        forward = [(i, i + 1) for i in range(count - 1)]
        if periodic:
            forward.append((count - 1, 0))
        backward = [(target, source) for source, target in forward]
        low = lax.ppermute(
            lax.slice_in_dim(block, block.shape[dim] - width, None, axis=dim), axis, forward
        )
        high = lax.ppermute(lax.slice_in_dim(block, 0, width, axis=dim), axis, backward)
        block = jnp.concatenate([low, block, high], axis=dim)
    return block


def cross_sum(padded):
    inner_y, inner_x = (padded.shape[0] - 2, padded.shape[1] - 2)
    middle_rows = lax.slice_in_dim(padded, 1, 1 + inner_y, axis=0)
    middle_columns = lax.slice_in_dim(padded, 1, 1 + inner_x, axis=1)
    return (
        lax.slice_in_dim(middle_columns, 0, inner_y, axis=0)
        + lax.slice_in_dim(middle_columns, 2, 2 + inner_y, axis=0)
        + lax.slice_in_dim(middle_rows, 0, inner_x, axis=1)
        + lax.slice_in_dim(middle_rows, 2, 2 + inner_x, axis=1)
    )


def smooth_step(padded, values, load, mass_here):
    return values + 0.8 * (load + cross_sum(padded) - (4.0 + mass_here) * values) / (
        4.0 + mass_here
    )


def block_means(values):
    cut = values.reshape(
        values.shape[0] // RATIO, RATIO, values.shape[1] // RATIO, RATIO, values.shape[2]
    )
    return jnp.mean(cut, axis=(1, 3))


def spread_blocks(values):
    return jnp.repeat(jnp.repeat(values, RATIO, axis=0), RATIO, axis=1)


def strip_rim(values):
    return lax.slice_in_dim(
        lax.slice_in_dim(values, 1, values.shape[0] - 1, axis=0), 1, values.shape[1] - 1, axis=1
    )


def body(load_terms, start_values, reaction_rate):
    values = start_values
    for sweep in range(BEFORE):
        values = smooth_step(
            extended(values, (("band", 0), ("lane", 1)), 1, False),
            values,
            load_terms,
            reaction_rate,
        )
    defect = (
        load_terms
        + cross_sum(extended(values, (("band", 0), ("lane", 1)), 1, False))
        - (4.0 + reaction_rate) * values
    )
    coarse_load, coarse_mass = (block_means(defect) * RATIO, block_means(reaction_rate) * RATIO)
    coarse_values = 0.8 * coarse_load / (4.0 + coarse_mass)
    depth = 2
    load_mass = padded_2(
        jnp.concatenate([coarse_load, coarse_mass], axis=2), (("band", 0), ("lane", 1)), 2, False
    )
    wide_load, wide_mass = jnp.split(load_mass, 2, axis=2)
    place_y = (
        lax.axis_index("band") * coarse_load.shape[0]
        - depth
        + jnp.arange(coarse_load.shape[0] + 2 * depth)
    )
    place_x = (
        lax.axis_index("lane") * coarse_load.shape[1]
        - depth
        + jnp.arange(coarse_load.shape[1] + 2 * depth)
    )
    inside_y = (place_y >= 0) & (place_y < coarse_load.shape[0] * lax.axis_size("band"))
    inside_x = (place_x >= 0) & (place_x < coarse_load.shape[1] * lax.axis_size("lane"))
    inside = (inside_y[:, None] & inside_x[None, :])[:, :, None]
    for group in range((INNER - 1) // 2):
        wide_values = padded_2(coarse_values, (("band", 0), ("lane", 1)), 2, False)
        once = smooth_step(
            wide_values, strip_rim(wide_values), strip_rim(wide_load), strip_rim(wide_mass)
        )
        once = jnp.where(strip_rim(inside), once, 0.0)
        middle = strip_rim(once)
        coarse_values = smooth_step(once, middle, coarse_load, coarse_mass)
    values = values + spread_blocks(coarse_values)
    for sweep in range(AFTER):
        values = smooth_step(
            extended(values, (("band", 0), ("lane", 1)), 1, False),
            values,
            load_terms,
            reaction_rate,
        )
    solution = values
    remaining = (
        load_terms
        + cross_sum(extended(solution, (("band", 0), ("lane", 1)), 1, False))
        - (4.0 + reaction_rate) * solution
    )
    return (solution, remaining)


def solution(mesh):
    return jax.shard_map(
        body,
        mesh=mesh,
        in_specs=(P("band", "lane", None), P("band", "lane", None), P("band", "lane", None)),
        out_specs=(P("band", "lane", None), P("band", "lane", None)),
        check_vma=False,
    )
```

profile of v0, /device:TPU:109, one launch (start us, length us, event | category | flops | bytes accessed | tf_op | source)
XLA Modules:
  0.0 378.5 jit_solution(2018704563848098932)
XLA Ops:
  1.5 2.6 collective-permute-start.1
  4.1 6.6 %collective-permute-start = (f32[1,64,256]{2,1,0:T(8,128)S(1)}, f32[1,64,256]{2,1,0:T(8,128)S(1)}, u32[]{:S(2)}, u32[]{:S(2)}) collective-permute-start(f32[1,64,256]{2,1,0:T(8,128)S(1)} %get-tuple-element.32), channel_id=1, source_target_pairs={{0,8},{8,16},{16,24},{24,32},{32,40},{40,48},{48,56},{56,64},{64,7... | collective-permute-start | bytes 196616 | tf_op jit(solution)/shard_map/ppermute | solution.py:19
  12.0 2.8 collective-permute-start.2
  14.8 3.4 collective-permute-start.3
  18.3 3.1 constant_dynamic-update-slice_fusion.1
  23.0 6.5 %fusion.59 = f32[64,64,256]{2,1,0:T(8,128)S(1)} fusion(f32[64,64,256]{2,1,0:T(8,128)} %param.4, f32[64,64,256]{2,1,0:T(8,128)S(1)} %copy-done.2, f32[66,64,256]{2,1,0:T(8,128)S(1)} %constant_dynamic-update-slice_fusion, f32[64,1,256]{2,1,0:T(1,128)S(1)} %collective-permute-done.3, f32[64,1,256]{2,1,0:T(1,128)S(1)} %collective-permute-done.2, ...), kind=kLoop, calls=%fused_computation.108 | loop fusion | flops 20971520 | bytes 21364736 | tf_op jit(solution)/shard_map/add | solution.py:59
  31.6 4.1 %collective-permute-start.7 = (f32[64,1,256]{2,1,0:T(1,128)S(1)}, f32[64,1,256]{2,1,0:T(1,128)S(1)}, u32[]{:S(2)}, u32[]{:S(2)}) collective-permute-start(f32[64,1,256]{2,1,0:T(1,128)S(1)} %get-tuple-element.26), channel_id=1, source_target_pairs={{1,0},{2,1},{3,2},{4,3},{5,4},{6,5},{7,6},{9,8},{10,9},{11,10},{12... | collective-permute-start | bytes 196616 | tf_op jit(solution)/shard_map/ppermute | solution.py:19
  35.8 3.0 collective-permute-start.4
  40.9 7.2 %collective-permute-done.5 = f32[1,64,256]{2,1,0:T(8,128)S(1)} collective-permute-done((f32[1,64,256]{2,1,0:T(8,128)S(1)}, f32[1,64,256]{2,1,0:T(8,128)S(1)}, u32[]{:S(2)}, u32[]{:S(2)}) %collective-permute-start.5) | collective-permute-done | bytes 65568 | tf_op jit(solution)/shard_map/ppermute | solution.py:19
  48.0 5.7 %fusion.50 = f32[64,64,256]{2,1,0:T(8,128)S(1)} fusion(f32[64,64,256]{2,1,0:T(8,128)S(1)} %fusion.59, f32[64,64,256]{2,1,0:T(8,128)S(1)} %copy-done.2, f32[64,1,256]{2,1,0:T(1,128)S(1)} %collective-permute-done.7, f32[1,64,256]{2,1,0:T(8,128)S(1)} %collective-permute-done.5, f32[1,64,256]{2,1,0:T(8,128)S(1)} %collective-permute-done.4, ...), kind=kLoop, calls=%fused_computation.91 | loop fusion | flops 25165824 | bytes 17039360 | tf_op jit(solution)/shard_map/add | solution.py:59
  53.9 2.6 collective-permute-start.10
  56.4 3.6 collective-permute-start.11
  60.1 2.4 collective-permute-start.8
  64.5 7.2 %collective-permute-done.9 = f32[1,64,256]{2,1,0:T(8,128)S(1)} collective-permute-done((f32[1,64,256]{2,1,0:T(8,128)S(1)}, f32[1,64,256]{2,1,0:T(8,128)S(1)}, u32[]{:S(2)}, u32[]{:S(2)}) %collective-permute-start.9) | collective-permute-done | bytes 65568 | tf_op jit(solution)/shard_map/ppermute | solution.py:19
  71.7 5.7 %fusion.40 = f32[64,64,256]{2,1,0:T(8,128)S(1)} fusion(f32[64,64,256]{2,1,0:T(8,128)S(1)} %fusion.50, f32[64,64,256]{2,1,0:T(8,128)S(1)} %copy-done.2, f32[64,1,256]{2,1,0:T(1,128)S(1)} %collective-permute-done.11, f32[1,64,256]{2,1,0:T(8,128)S(1)} %collective-permute-done.9, f32[1,64,256]{2,1,0:T(8,128)S(1)} %collective-permute-done.8, ...), kind=kLoop, calls=%fused_computation.73 | loop fusion | flops 25165824 | bytes 17039360 | tf_op jit(solution)/shard_map/add | solution.py:59
  79.4 2.4 collective-permute-start.14
  81.8 3.8 %collective-permute-start.15 = (f32[64,1,256]{2,1,0:T(1,128)S(1)}, f32[64,1,256]{2,1,0:T(1,128)S(1)}, u32[]{:S(2)}, u32[]{:S(2)}) collective-permute-start(f32[64,1,256]{2,1,0:T(1,128)S(1)} %get-tuple-element.18), channel_id=1, source_target_pairs={{1,0},{2,1},{3,2},{4,3},{5,4},{6,5},{7,6},{9,8},{10,9},{11,10},{12... | collective-permute-start | bytes 196616 | tf_op jit(solution)/shard_map/ppermute | solution.py:19
  85.6 2.4 collective-permute-start.12
  90.3 5.8 %reshape.32 = f32[32,2,32,2,256]{4,3,2,1,0:T(2,128)} reshape(f32[64,64,256]{2,1,0:T(8,128)} %param.5) | data formatting | bytes 8388608 | tf_op jit(solution)/shard_map/reshape | solution.py:65
  96.1 5.5 %reduce_sum.19 = f32[32,32,256]{2,1,0:T(8,128)S(1)} reduce(f32[32,2,32,2,256]{4,3,2,1,0:T(2,128)} %reshape.32, f32[]{:T(128)} %constant.13.clone.1), dimensions={1,3}, to_apply=%region_1.2 | reduce | flops 786432 | bytes 5242884 | tf_op jit(solution)/shard_map/reduce_sum | solution.py:68
  101.6 13.6 %fusion.30 = f32[64,64,256]{2,1,0:T(8,128)} fusion(f32[64,64,256]{2,1,0:T(8,128)} %param.3, f32[64,1,256]{2,1,0:T(1,128)S(1)} %collective-permute-done.15, f32[1,64,256]{2,1,0:T(8,128)S(1)} %collective-permute-done.13, f32[64,64,256]{2,1,0:T(8,128)} %copy-done.4, f32[1,64,256]{2,1,0:T(8,128)S(1)} %collective-permute-done.12, ...), kind=kLoop, calls=%fused_computation.55 | loop fusion | flops 22020096 | bytes 17039360 | tf_op jit(solution)/shard_map/sub | solution.py:91
  115.2 5.8 %reshape.31 = f32[32,2,32,2,256]{4,3,2,1,0:T(2,128)} reshape(f32[64,64,256]{2,1,0:T(8,128)} %fusion.30) | data formatting | bytes 8388608 | tf_op jit(solution)/shard_map/reshape | solution.py:65
  121.0 5.5 %reduce_sum.18 = f32[32,32,256]{2,1,0:T(8,128)S(1)} reduce(f32[32,2,32,2,256]{4,3,2,1,0:T(2,128)} %reshape.31, f32[]{:T(128)} %constant.13.clone.1), dimensions={1,3}, to_apply=%region_0.1 | reduce | flops 786432 | bytes 5242884 | tf_op jit(solution)/shard_map/reduce_sum | solution.py:68
  126.9 7.3 %collective-permute-start.16 = (f32[2,32,256]{2,1,0:T(8,128)S(1)}, f32[2,32,256]{2,1,0:T(8,128)S(1)}, u32[]{:S(2)}, u32[]{:S(2)}) collective-permute-start(f32[2,32,256]{2,1,0:T(8,128)S(1)} %get-tuple-element.62), channel_id=1, source_target_pairs={{0,8},{8,16},{16,24},{24,32},{32,40},{40,48},{48,56},{56,64},{64,7... | collective-permute-start | bytes 196616 | tf_op jit(solution)/shard_map/ppermute | solution.py:38
  136.2 7.3 %collective-permute-start.20 = (f32[2,32,512]{2,1,0:T(8,128)S(1)}, f32[2,32,512]{2,1,0:T(8,128)S(1)}, u32[]{:S(2)}, u32[]{:S(2)}) collective-permute-start(f32[2,32,512]{2,1,0:T(8,128)S(1)} %get-tuple-element.35), channel_id=1, source_target_pairs={{0,8},{8,16},{16,24},{24,32},{32,40},{40,48},{48,56},{56,64},{64,7... | collective-permute-start | bytes 393224 | tf_op jit(solution)/shard_map/ppermute | solution.py:38
  145.5 2.4 collective-permute-start.18
  147.9 3.8 %collective-permute-start.19 = (f32[36,2,256]{2,1,0:T(2,128)S(1)}, f32[36,2,256]{2,1,0:T(2,128)S(1)}, u32[]{:S(2)}, u32[]{:S(2)}) collective-permute-start(f32[36,2,256]{2,1,0:T(2,128)S(1)} %get-tuple-element.48), channel_id=1, source_target_pairs={{1,0},{2,1},{3,2},{4,3},{5,4},{6,5},{7,6},{9,8},{10,9},{11,10},{12... | collective-permute-start | bytes 221192 | tf_op jit(solution)/shard_map/ppermute | solution.py:41
  155.8 4.0 %collective-permute-start.23 = (f32[36,2,512]{2,1,0:T(2,128)S(1)}, f32[36,2,512]{2,1,0:T(2,128)S(1)}, u32[]{:S(2)}, u32[]{:S(2)}) collective-permute-start(f32[36,2,512]{2,1,0:T(2,128)S(1)} %get-tuple-element.34), channel_id=1, source_target_pairs={{1,0},{2,1},{3,2},{4,3},{5,4},{6,5},{7,6},{9,8},{10,9},{11,10},{12... | collective-permute-start | bytes 442376 | tf_op jit(solution)/shard_map/ppermute | solution.py:41
  162.3 3.8 fusion.105
  166.8 7.4 %collective-permute-start.24 = (f32[2,32,256]{2,1,0:T(8,128)S(1)}, f32[2,32,256]{2,1,0:T(8,128)S(1)}, u32[]{:S(2)}, u32[]{:S(2)}) collective-permute-start(f32[2,32,256]{2,1,0:T(8,128)S(1)} %get-tuple-element.57), channel_id=1, source_target_pairs={{0,8},{8,16},{16,24},{24,32},{32,40},{40,48},{48,56},{56,64},{64,7... | collective-permute-start | bytes 196616 | tf_op jit(solution)/shard_map/ppermute | solution.py:38
  176.1 7.3 %collective-permute-done.25 = f32[2,32,256]{2,1,0:T(8,128)S(1)} collective-permute-done((f32[2,32,256]{2,1,0:T(8,128)S(1)}, f32[2,32,256]{2,1,0:T(8,128)S(1)}, u32[]{:S(2)}, u32[]{:S(2)}) %collective-permute-start.25) | collective-permute-done | bytes 65568 | tf_op jit(solution)/shard_map/ppermute | solution.py:41
  183.4 5.1 %collective-permute-start.26 = (f32[36,2,256]{2,1,0:T(2,128)S(1)}, f32[36,2,256]{2,1,0:T(2,128)S(1)}, u32[]{:S(2)}, u32[]{:S(2)}) collective-permute-start(f32[36,2,256]{2,1,0:T(2,128)S(1)} %get-tuple-element.45), channel_id=1, source_target_pairs={{0,1},{1,2},{2,3},{3,4},{4,5},{5,6},{6,7},{8,9},{9,10},{10,11},{11... | collective-permute-start | bytes 221192 | tf_op jit(solution)/shard_map/ppermute | solution.py:38
  190.5 3.2 collective-permute-done.27
  196.4 3.3 collective-permute-start.28
  201.6 7.3 %collective-permute-done.29 = f32[2,32,256]{2,1,0:T(8,128)S(1)} collective-permute-done((f32[2,32,256]{2,1,0:T(8,128)S(1)}, f32[2,32,256]{2,1,0:T(8,128)S(1)}, u32[]{:S(2)}, u32[]{:S(2)}) %collective-permute-start.29) | collective-permute-done | bytes 65568 | tf_op jit(solution)/shard_map/ppermute | solution.py:41
  208.9 2.6 collective-permute-start.30
  211.5 3.6 collective-permute-start.31
  219.5 2.9 collective-permute-start.32
  224.4 7.3 %collective-permute-done.33 = f32[2,32,256]{2,1,0:T(8,128)S(1)} collective-permute-done((f32[2,32,256]{2,1,0:T(8,128)S(1)}, f32[2,32,256]{2,1,0:T(8,128)S(1)}, u32[]{:S(2)}, u32[]{:S(2)}) %collective-permute-start.33) | collective-permute-done | bytes 65568 | tf_op jit(solution)/shard_map/ppermute | solution.py:41
  231.7 5.1 %collective-permute-start.34 = (f32[36,2,256]{2,1,0:T(2,128)S(1)}, f32[36,2,256]{2,1,0:T(2,128)S(1)}, u32[]{:S(2)}, u32[]{:S(2)}) collective-permute-start(f32[36,2,256]{2,1,0:T(2,128)S(1)} %get-tuple-element.41), channel_id=1, source_target_pairs={{0,1},{1,2},{2,3},{3,4},{4,5},{5,6},{6,7},{8,9},{9,10},{10,11},{11... | collective-permute-start | bytes 221192 | tf_op jit(solution)/shard_map/ppermute | solution.py:38
  238.9 3.0 collective-permute-done.35
  244.7 3.3 collective-permute-start.36
  249.9 7.3 %collective-permute-done.37 = f32[2,32,256]{2,1,0:T(8,128)S(1)} collective-permute-done((f32[2,32,256]{2,1,0:T(8,128)S(1)}, f32[2,32,256]{2,1,0:T(8,128)S(1)}, u32[]{:S(2)}, u32[]{:S(2)}) %collective-permute-start.37) | collective-permute-done | bytes 65568 | tf_op jit(solution)/shard_map/ppermute | solution.py:41
  257.2 2.6 collective-permute-start.38
  259.8 3.6 collective-permute-start.39
  268.3 2.6 collective-permute-start.40
  272.9 7.3 %collective-permute-done.41 = f32[2,32,256]{2,1,0:T(8,128)S(1)} collective-permute-done((f32[2,32,256]{2,1,0:T(8,128)S(1)}, f32[2,32,256]{2,1,0:T(8,128)S(1)}, u32[]{:S(2)}, u32[]{:S(2)}) %collective-permute-start.41) | collective-permute-done | bytes 65568 | tf_op jit(solution)/shard_map/ppermute | solution.py:41
  280.2 2.6 collective-permute-start.42
  282.7 4.7 %collective-permute-start.43 = (f32[36,2,256]{2,1,0:T(2,128)S(1)}, f32[36,2,256]{2,1,0:T(2,128)S(1)}, u32[]{:S(2)}, u32[]{:S(2)}) collective-permute-start(f32[36,2,256]{2,1,0:T(2,128)S(1)} %get-tuple-element.38), channel_id=1, source_target_pairs={{1,0},{2,1},{3,2},{4,3},{5,4},{6,5},{7,6},{9,8},{10,9},{11,10},{12... | collective-permute-start | bytes 221192 | tf_op jit(solution)/shard_map/ppermute | solution.py:41
  291.6 3.5 broadcast_in_dim.47
  295.1 6.1 %reshape.34 = f32[64,64,256]{2,1,0:T(8,128)} reshape(f32[64,32,2,256]{3,2,1,0:T(2,128)} %broadcast_in_dim.47) | data formatting | bytes 8388608 | tf_op jit(solution)/shard_map/reshape | solution.py:72
  301.2 4.4 %add.461 = f32[64,64,256]{2,1,0:T(8,128)S(1)} add(f32[64,64,256]{2,1,0:T(8,128)} %copy-done.4, f32[64,64,256]{2,1,0:T(8,128)} %reshape.34) | non-fusion elementwise | flops 1048576 | bytes 12582912 | tf_op jit(solution)/shard_map/add | solution.py:123
  307.9 4.5 %collective-permute-start.47 = (f32[64,1,256]{2,1,0:T(1,128)S(1)}, f32[64,1,256]{2,1,0:T(1,128)S(1)}, u32[]{:S(2)}, u32[]{:S(2)}) collective-permute-start(f32[64,1,256]{2,1,0:T(1,128)S(1)} %get-tuple-element.14), channel_id=1, source_target_pairs={{1,0},{2,1},{3,2},{4,3},{5,4},{6,5},{7,6},{9,8},{10,9},{11,10},{12... | collective-permute-start | bytes 196616 | tf_op jit(solution)/shard_map/ppermute | solution.py:19
  312.4 2.7 collective-permute-start.44
  317.0 7.2 %collective-permute-done.45 = f32[1,64,256]{2,1,0:T(8,128)S(1)} collective-permute-done((f32[1,64,256]{2,1,0:T(8,128)S(1)}, f32[1,64,256]{2,1,0:T(8,128)S(1)}, u32[]{:S(2)}, u32[]{:S(2)}) %collective-permute-start.45) | collective-permute-done | bytes 65568 | tf_op jit(solution)/shard_map/ppermute | solution.py:19
  324.3 5.7 %fusion.23 = f32[64,64,256]{2,1,0:T(8,128)S(1)} fusion(f32[64,64,256]{2,1,0:T(8,128)S(1)} %add.461, f32[64,64,256]{2,1,0:T(8,128)S(1)} %copy-done.3, f32[64,1,256]{2,1,0:T(1,128)S(1)} %collective-permute-done.47, f32[1,64,256]{2,1,0:T(8,128)S(1)} %collective-permute-done.45, f32[1,64,256]{2,1,0:T(8,128)S(1)} %collective-permute-done.44, ...), kind=kLoop, calls=%fused_computation.40 | loop fusion | flops 25165824 | bytes 17039360 | tf_op jit(solution)/shard_map/add | solution.py:59
  332.0 4.3 %collective-permute-start.51 = (f32[64,1,256]{2,1,0:T(1,128)S(1)}, f32[64,1,256]{2,1,0:T(1,128)S(1)}, u32[]{:S(2)}, u32[]{:S(2)}) collective-permute-start(f32[64,1,256]{2,1,0:T(1,128)S(1)} %get-tuple-element.10), channel_id=1, source_target_pairs={{1,0},{2,1},{3,2},{4,3},{5,4},{6,5},{7,6},{9,8},{10,9},{11,10},{12... | collective-permute-start | bytes 196616 | tf_op jit(solution)/shard_map/ppermute | solution.py:19
  336.3 2.4 collective-permute-start.48
  340.7 7.2 %collective-permute-done.49 = f32[1,64,256]{2,1,0:T(8,128)S(1)} collective-permute-done((f32[1,64,256]{2,1,0:T(8,128)S(1)}, f32[1,64,256]{2,1,0:T(8,128)S(1)}, u32[]{:S(2)}, u32[]{:S(2)}) %collective-permute-start.49) | collective-permute-done | bytes 65568 | tf_op jit(solution)/shard_map/ppermute | solution.py:19
  347.9 5.7 %fusion.13 = f32[64,64,256]{2,1,0:T(8,128)S(1)} fusion(f32[64,64,256]{2,1,0:T(8,128)S(1)} %fusion.23, f32[64,64,256]{2,1,0:T(8,128)S(1)} %copy-done.3, f32[64,1,256]{2,1,0:T(1,128)S(1)} %collective-permute-done.51, f32[1,64,256]{2,1,0:T(8,128)S(1)} %collective-permute-done.49, f32[1,64,256]{2,1,0:T(8,128)S(1)} %collective-permute-done.48, ...), kind=kLoop, calls=%fused_computation.22 | loop fusion | flops 25165824 | bytes 17039360 | tf_op jit(solution)/shard_map/add | solution.py:59
  355.7 4.3 %collective-permute-start.55 = (f32[64,1,256]{2,1,0:T(1,128)S(1)}, f32[64,1,256]{2,1,0:T(1,128)S(1)}, u32[]{:S(2)}, u32[]{:S(2)}) collective-permute-start(f32[64,1,256]{2,1,0:T(1,128)S(1)} %get-tuple-element.6), channel_id=1, source_target_pairs={{1,0},{2,1},{3,2},{4,3},{5,4},{6,5},{7,6},{9,8},{10,9},{11,10},{12... | collective-permute-start | bytes 196616 | tf_op jit(solution)/shard_map/ppermute | solution.py:19
  360.0 2.4 collective-permute-start.52
  364.4 7.2 %collective-permute-done.53 = f32[1,64,256]{2,1,0:T(8,128)S(1)} collective-permute-done((f32[1,64,256]{2,1,0:T(8,128)S(1)}, f32[1,64,256]{2,1,0:T(8,128)S(1)}, u32[]{:S(2)}, u32[]{:S(2)}) %collective-permute-start.53) | collective-permute-done | bytes 65568 | tf_op jit(solution)/shard_map/ppermute | solution.py:19
  371.6 6.4 %fusion.3 = f32[64,64,256]{2,1,0:T(8,128)} fusion(f32[64,64,256]{2,1,0:T(8,128)S(1)} %copy-done.3, f32[64,1,256]{2,1,0:T(1,128)S(1)} %collective-permute-done.55, f32[1,64,256]{2,1,0:T(8,128)S(1)} %collective-permute-done.53, f32[64,64,256]{2,1,0:T(8,128)S(1)} %fusion.13, f32[1,64,256]{2,1,0:T(8,128)S(1)} %collective-permute-done.52, ...), kind=kLoop, calls=%fused_computation.4 | loop fusion | flops 22020096 | bytes 17039360 | tf_op jit(solution)/shard_map/sub | solution.py:133
  (130 shorter events, 70.5 us)
Async XLA Ops:
  1.5 19.9 %collective-permute-start.1 = (f32[1,64,256]{2,1,0:T(8,128)S(1)}, f32[1,64,256]{2,1,0:T(8,128)S(1)}, u32[]{:S(2)}, u32[]{:S(2)}) collective-permute-start(f32[1,64,256]{2,1,0:T(8,128)S(1)} %get-tuple-element.31), channel_id=1, source_target_pairs={{8,0},{16,8},{24,16},{32,24},{40,32},{48,40},{56,48},{64,56},{72,6... | collective-permute-start | bytes 196616 | tf_op jit(solution)/shard_map/ppermute | solution.py:19
  4.1 14.1 %collective-permute-start = (f32[1,64,256]{2,1,0:T(8,128)S(1)}, f32[1,64,256]{2,1,0:T(8,128)S(1)}, u32[]{:S(2)}, u32[]{:S(2)}) collective-permute-start(f32[1,64,256]{2,1,0:T(8,128)S(1)} %get-tuple-element.32), channel_id=1, source_target_pairs={{0,8},{8,16},{16,24},{24,32},{32,40},{40,48},{48,56},{56,64},{64,7... | collective-permute-start | bytes 196616 | tf_op jit(solution)/shard_map/ppermute | solution.py:19
  12.0 9.4 %collective-permute-start.2 = (f32[64,1,256]{2,1,0:T(1,128)S(1)}, f32[64,1,256]{2,1,0:T(1,128)S(1)}, u32[]{:S(2)}, u32[]{:S(2)}) collective-permute-start(f32[64,1,256]{2,1,0:T(1,128)S(1)} %get-tuple-element.29), channel_id=1, source_target_pairs={{0,1},{1,2},{2,3},{3,4},{4,5},{5,6},{6,7},{8,9},{9,10},{10,11},{11... | collective-permute-start | bytes 196616 | tf_op jit(solution)/shard_map/ppermute | solution.py:19
  14.8 6.6 %collective-permute-start.3 = (f32[64,1,256]{2,1,0:T(1,128)S(1)}, f32[64,1,256]{2,1,0:T(1,128)S(1)}, u32[]{:S(2)}, u32[]{:S(2)}) collective-permute-start(f32[64,1,256]{2,1,0:T(1,128)S(1)} %get-tuple-element.30), channel_id=1, source_target_pairs={{1,0},{2,1},{3,2},{4,3},{5,4},{6,5},{7,6},{9,8},{10,9},{11,10},{12... | collective-permute-start | bytes 196616 | tf_op jit(solution)/shard_map/ppermute | solution.py:19
  18.2 3.5 copy-start
  18.3 4.7 %copy-start.2 = (f32[64,64,256]{2,1,0:T(8,128)S(1)}, f32[64,64,256]{2,1,0:T(8,128)}, u32[]{:S(2)}) copy-start(f32[64,64,256]{2,1,0:T(8,128)} %param.3) | copy-start | bytes 12582916
  29.6 11.3 %collective-permute-start.6 = (f32[64,1,256]{2,1,0:T(1,128)S(1)}, f32[64,1,256]{2,1,0:T(1,128)S(1)}, u32[]{:S(2)}, u32[]{:S(2)}) collective-permute-start(f32[64,1,256]{2,1,0:T(1,128)S(1)} %get-tuple-element.25), channel_id=1, source_target_pairs={{0,1},{1,2},{2,3},{3,4},{4,5},{5,6},{6,7},{8,9},{9,10},{10,11},{11... | collective-permute-start | bytes 196616 | tf_op jit(solution)/shard_map/ppermute | solution.py:19
  31.6 9.2 %collective-permute-start.7 = (f32[64,1,256]{2,1,0:T(1,128)S(1)}, f32[64,1,256]{2,1,0:T(1,128)S(1)}, u32[]{:S(2)}, u32[]{:S(2)}) collective-permute-start(f32[64,1,256]{2,1,0:T(1,128)S(1)} %get-tuple-element.26), channel_id=1, source_target_pairs={{1,0},{2,1},{3,2},{4,3},{5,4},{6,5},{7,6},{9,8},{10,9},{11,10},{12... | collective-permute-start | bytes 196616 | tf_op jit(solution)/shard_map/ppermute | solution.py:19
  35.8 5.1 %collective-permute-start.4 = (f32[1,64,256]{2,1,0:T(8,128)S(1)}, f32[1,64,256]{2,1,0:T(8,128)S(1)}, u32[]{:S(2)}, u32[]{:S(2)}) collective-permute-start(f32[1,64,256]{2,1,0:T(8,128)S(1)} %get-tuple-element.27), channel_id=1, source_target_pairs={{0,8},{8,16},{16,24},{24,32},{32,40},{40,48},{48,56},{56,64},{64,7... | collective-permute-start | bytes 196616 | tf_op jit(solution)/shard_map/ppermute | solution.py:19
  38.8 9.2 %collective-permute-start.5 = (f32[1,64,256]{2,1,0:T(8,128)S(1)}, f32[1,64,256]{2,1,0:T(8,128)S(1)}, u32[]{:S(2)}, u32[]{:S(2)}) collective-permute-start(f32[1,64,256]{2,1,0:T(8,128)S(1)} %get-tuple-element.28), channel_id=1, source_target_pairs={{8,0},{16,8},{24,16},{32,24},{40,32},{48,40},{56,48},{64,56},{72,6... | collective-permute-start | bytes 196616 | tf_op jit(solution)/shard_map/ppermute | solution.py:19
  53.9 10.6 %collective-permute-start.10 = (f32[64,1,256]{2,1,0:T(1,128)S(1)}, f32[64,1,256]{2,1,0:T(1,128)S(1)}, u32[]{:S(2)}, u32[]{:S(2)}) collective-permute-start(f32[64,1,256]{2,1,0:T(1,128)S(1)} %get-tuple-element.21), channel_id=1, source_target_pairs={{0,1},{1,2},{2,3},{3,4},{4,5},{5,6},{6,7},{8,9},{9,10},{10,11},{11... | collective-permute-start | bytes 196616 | tf_op jit(solution)/shard_map/ppermute | solution.py:19
  56.4 8.0 %collective-permute-start.11 = (f32[64,1,256]{2,1,0:T(1,128)S(1)}, f32[64,1,256]{2,1,0:T(1,128)S(1)}, u32[]{:S(2)}, u32[]{:S(2)}) collective-permute-start(f32[64,1,256]{2,1,0:T(1,128)S(1)} %get-tuple-element.22), channel_id=1, source_target_pairs={{1,0},{2,1},{3,2},{4,3},{5,4},{6,5},{7,6},{9,8},{10,9},{11,10},{12... | collective-permute-start | bytes 196616 | tf_op jit(solution)/shard_map/ppermute | solution.py:19
  60.1 4.4 %collective-permute-start.8 = (f32[1,64,256]{2,1,0:T(8,128)S(1)}, f32[1,64,256]{2,1,0:T(8,128)S(1)}, u32[]{:S(2)}, u32[]{:S(2)}) collective-permute-start(f32[1,64,256]{2,1,0:T(8,128)S(1)} %get-tuple-element.23), channel_id=1, source_target_pairs={{0,8},{8,16},{16,24},{24,32},{32,40},{40,48},{48,56},{56,64},{64,7... | collective-permute-start | bytes 196616 | tf_op jit(solution)/shard_map/ppermute | solution.py:19
  62.5 9.2 %collective-permute-start.9 = (f32[1,64,256]{2,1,0:T(8,128)S(1)}, f32[1,64,256]{2,1,0:T(8,128)S(1)}, u32[]{:S(2)}, u32[]{:S(2)}) collective-permute-start(f32[1,64,256]{2,1,0:T(8,128)S(1)} %get-tuple-element.24), channel_id=1, source_target_pairs={{8,0},{16,8},{24,16},{32,24},{40,32},{48,40},{56,48},{64,56},{72,6... | collective-permute-start | bytes 196616 | tf_op jit(solution)/shard_map/ppermute | solution.py:19
  77.4 2.0 copy-start.4
  79.4 22.1 %collective-permute-start.14 = (f32[64,1,256]{2,1,0:T(1,128)S(1)}, f32[64,1,256]{2,1,0:T(1,128)S(1)}, u32[]{:S(2)}, u32[]{:S(2)}) collective-permute-start(f32[64,1,256]{2,1,0:T(1,128)S(1)} %get-tuple-element.17), channel_id=1, source_target_pairs={{0,1},{1,2},{2,3},{3,4},{4,5},{5,6},{6,7},{8,9},{9,10},{10,11},{11... | collective-permute-start | bytes 196616 | tf_op jit(solution)/shard_map/ppermute | solution.py:19
  81.8 19.8 %collective-permute-start.15 = (f32[64,1,256]{2,1,0:T(1,128)S(1)}, f32[64,1,256]{2,1,0:T(1,128)S(1)}, u32[]{:S(2)}, u32[]{:S(2)}) collective-permute-start(f32[64,1,256]{2,1,0:T(1,128)S(1)} %get-tuple-element.18), channel_id=1, source_target_pairs={{1,0},{2,1},{3,2},{4,3},{5,4},{6,5},{7,6},{9,8},{10,9},{11,10},{12... | collective-permute-start | bytes 196616 | tf_op jit(solution)/shard_map/ppermute | solution.py:19
  85.6 15.9 %collective-permute-start.12 = (f32[1,64,256]{2,1,0:T(8,128)S(1)}, f32[1,64,256]{2,1,0:T(8,128)S(1)}, u32[]{:S(2)}, u32[]{:S(2)}) collective-permute-start(f32[1,64,256]{2,1,0:T(8,128)S(1)} %get-tuple-element.19), channel_id=1, source_target_pairs={{0,8},{8,16},{16,24},{24,32},{32,40},{40,48},{48,56},{56,64},{64,7... | collective-permute-start | bytes 196616 | tf_op jit(solution)/shard_map/ppermute | solution.py:19
  88.1 13.5 %collective-permute-start.13 = (f32[1,64,256]{2,1,0:T(8,128)S(1)}, f32[1,64,256]{2,1,0:T(8,128)S(1)}, u32[]{:S(2)}, u32[]{:S(2)}) collective-permute-start(f32[1,64,256]{2,1,0:T(8,128)S(1)} %get-tuple-element.20), channel_id=1, source_target_pairs={{8,0},{16,8},{24,16},{32,24},{40,32},{48,40},{56,48},{64,56},{72,6... | collective-permute-start | bytes 196616 | tf_op jit(solution)/shard_map/ppermute | solution.py:19
  126.9 18.5 %collective-permute-start.16 = (f32[2,32,256]{2,1,0:T(8,128)S(1)}, f32[2,32,256]{2,1,0:T(8,128)S(1)}, u32[]{:S(2)}, u32[]{:S(2)}) collective-permute-start(f32[2,32,256]{2,1,0:T(8,128)S(1)} %get-tuple-element.62), channel_id=1, source_target_pairs={{0,8},{8,16},{16,24},{24,32},{32,40},{40,48},{48,56},{56,64},{64,7... | collective-permute-start | bytes 196616 | tf_op jit(solution)/shard_map/ppermute | solution.py:38
  134.2 11.2 %collective-permute-start.17 = (f32[2,32,256]{2,1,0:T(8,128)S(1)}, f32[2,32,256]{2,1,0:T(8,128)S(1)}, u32[]{:S(2)}, u32[]{:S(2)}) collective-permute-start(f32[2,32,256]{2,1,0:T(8,128)S(1)} %get-tuple-element.63), channel_id=1, source_target_pairs={{8,0},{16,8},{24,16},{32,24},{40,32},{48,40},{56,48},{64,56},{72,6... | collective-permute-start | bytes 196616 | tf_op jit(solution)/shard_map/ppermute | solution.py:41
  136.2 15.5 %collective-permute-start.20 = (f32[2,32,512]{2,1,0:T(8,128)S(1)}, f32[2,32,512]{2,1,0:T(8,128)S(1)}, u32[]{:S(2)}, u32[]{:S(2)}) collective-permute-start(f32[2,32,512]{2,1,0:T(8,128)S(1)} %get-tuple-element.35), channel_id=1, source_target_pairs={{0,8},{8,16},{16,24},{24,32},{32,40},{40,48},{48,56},{56,64},{64,7... | collective-permute-start | bytes 393224 | tf_op jit(solution)/shard_map/ppermute | solution.py:38
  143.4 9.9 %collective-permute-start.21 = (f32[2,32,512]{2,1,0:T(8,128)S(1)}, f32[2,32,512]{2,1,0:T(8,128)S(1)}, u32[]{:S(2)}, u32[]{:S(2)}) collective-permute-start(f32[2,32,512]{2,1,0:T(8,128)S(1)} %get-tuple-element.36), channel_id=1, source_target_pairs={{8,0},{16,8},{24,16},{32,24},{40,32},{48,40},{56,48},{64,56},{72,6... | collective-permute-start | bytes 393224 | tf_op jit(solution)/shard_map/ppermute | solution.py:41
  145.5 14.4 %collective-permute-start.18 = (f32[36,2,256]{2,1,0:T(2,128)S(1)}, f32[36,2,256]{2,1,0:T(2,128)S(1)}, u32[]{:S(2)}, u32[]{:S(2)}) collective-permute-start(f32[36,2,256]{2,1,0:T(2,128)S(1)} %get-tuple-element.47), channel_id=1, source_target_pairs={{0,1},{1,2},{2,3},{3,4},{4,5},{5,6},{6,7},{8,9},{9,10},{10,11},{11... | collective-permute-start | bytes 221192 | tf_op jit(solution)/shard_map/ppermute | solution.py:38
  147.9 12.0 %collective-permute-start.19 = (f32[36,2,256]{2,1,0:T(2,128)S(1)}, f32[36,2,256]{2,1,0:T(2,128)S(1)}, u32[]{:S(2)}, u32[]{:S(2)}) collective-permute-start(f32[36,2,256]{2,1,0:T(2,128)S(1)} %get-tuple-element.48), channel_id=1, source_target_pairs={{1,0},{2,1},{3,2},{4,3},{5,4},{6,5},{7,6},{9,8},{10,9},{11,10},{12... | collective-permute-start | bytes 221192 | tf_op jit(solution)/shard_map/ppermute | solution.py:41
  153.4 6.8 %collective-permute-start.22 = (f32[36,2,512]{2,1,0:T(2,128)S(1)}, f32[36,2,512]{2,1,0:T(2,128)S(1)}, u32[]{:S(2)}, u32[]{:S(2)}) collective-permute-start(f32[36,2,512]{2,1,0:T(2,128)S(1)} %get-tuple-element.33), channel_id=1, source_target_pairs={{0,1},{1,2},{2,3},{3,4},{4,5},{5,6},{6,7},{8,9},{9,10},{10,11},{11... | collective-permute-start | bytes 442376 | tf_op jit(solution)/shard_map/ppermute | solution.py:38
  155.8 6.5 %collective-permute-start.23 = (f32[36,2,512]{2,1,0:T(2,128)S(1)}, f32[36,2,512]{2,1,0:T(2,128)S(1)}, u32[]{:S(2)}, u32[]{:S(2)}) collective-permute-start(f32[36,2,512]{2,1,0:T(2,128)S(1)} %get-tuple-element.34), channel_id=1, source_target_pairs={{1,0},{2,1},{3,2},{4,3},{5,4},{6,5},{7,6},{9,8},{10,9},{11,10},{12... | collective-permute-start | bytes 442376 | tf_op jit(solution)/shard_map/ppermute | solution.py:41
  166.8 9.3 %collective-permute-start.24 = (f32[2,32,256]{2,1,0:T(8,128)S(1)}, f32[2,32,256]{2,1,0:T(8,128)S(1)}, u32[]{:S(2)}, u32[]{:S(2)}) collective-permute-start(f32[2,32,256]{2,1,0:T(8,128)S(1)} %get-tuple-element.57), channel_id=1, source_target_pairs={{0,8},{8,16},{16,24},{24,32},{32,40},{40,48},{48,56},{56,64},{64,7... | collective-permute-start | bytes 196616 | tf_op jit(solution)/shard_map/ppermute | solution.py:38
  174.1 9.2 %collective-permute-start.25 = (f32[2,32,256]{2,1,0:T(8,128)S(1)}, f32[2,32,256]{2,1,0:T(8,128)S(1)}, u32[]{:S(2)}, u32[]{:S(2)}) collective-permute-start(f32[2,32,256]{2,1,0:T(8,128)S(1)} %get-tuple-element.58), channel_id=1, source_target_pairs={{8,0},{16,8},{24,16},{32,24},{40,32},{48,40},{56,48},{64,56},{72,6... | collective-permute-start | bytes 196616 | tf_op jit(solution)/shard_map/ppermute | solution.py:41
  183.4 7.1 %collective-permute-start.26 = (f32[36,2,256]{2,1,0:T(2,128)S(1)}, f32[36,2,256]{2,1,0:T(2,128)S(1)}, u32[]{:S(2)}, u32[]{:S(2)}) collective-permute-start(f32[36,2,256]{2,1,0:T(2,128)S(1)} %get-tuple-element.45), channel_id=1, source_target_pairs={{0,1},{1,2},{2,3},{3,4},{4,5},{5,6},{6,7},{8,9},{9,10},{10,11},{11... | collective-permute-start | bytes 221192 | tf_op jit(solution)/shard_map/ppermute | solution.py:38
  188.5 5.1 %collective-permute-start.27 = (f32[36,2,256]{2,1,0:T(2,128)S(1)}, f32[36,2,256]{2,1,0:T(2,128)S(1)}, u32[]{:S(2)}, u32[]{:S(2)}) collective-permute-start(f32[36,2,256]{2,1,0:T(2,128)S(1)} %get-tuple-element.46), channel_id=1, source_target_pairs={{1,0},{2,1},{3,2},{4,3},{5,4},{6,5},{7,6},{9,8},{10,9},{11,10},{12... | collective-permute-start | bytes 221192 | tf_op jit(solution)/shard_map/ppermute | solution.py:41
  196.4 5.2 %collective-permute-start.28 = (f32[2,32,256]{2,1,0:T(8,128)S(1)}, f32[2,32,256]{2,1,0:T(8,128)S(1)}, u32[]{:S(2)}, u32[]{:S(2)}) collective-permute-start(f32[2,32,256]{2,1,0:T(8,128)S(1)} %get-tuple-element.55), channel_id=1, source_target_pairs={{0,8},{8,16},{16,24},{24,32},{32,40},{40,48},{48,56},{56,64},{64,7... | collective-permute-start | bytes 196616 | tf_op jit(solution)/shard_map/ppermute | solution.py:38
  199.7 9.2 %collective-permute-start.29 = (f32[2,32,256]{2,1,0:T(8,128)S(1)}, f32[2,32,256]{2,1,0:T(8,128)S(1)}, u32[]{:S(2)}, u32[]{:S(2)}) collective-permute-start(f32[2,32,256]{2,1,0:T(8,128)S(1)} %get-tuple-element.56), channel_id=1, source_target_pairs={{8,0},{16,8},{24,16},{32,24},{40,32},{48,40},{56,48},{64,56},{72,6... | collective-permute-start | bytes 196616 | tf_op jit(solution)/shard_map/ppermute | solution.py:41
  208.9 6.2 %collective-permute-start.30 = (f32[36,2,256]{2,1,0:T(2,128)S(1)}, f32[36,2,256]{2,1,0:T(2,128)S(1)}, u32[]{:S(2)}, u32[]{:S(2)}) collective-permute-start(f32[36,2,256]{2,1,0:T(2,128)S(1)} %get-tuple-element.43), channel_id=1, source_target_pairs={{0,1},{1,2},{2,3},{3,4},{4,5},{5,6},{6,7},{8,9},{9,10},{10,11},{11... | collective-permute-start | bytes 221192 | tf_op jit(solution)/shard_map/ppermute | solution.py:38
  211.5 5.3 %collective-permute-start.31 = (f32[36,2,256]{2,1,0:T(2,128)S(1)}, f32[36,2,256]{2,1,0:T(2,128)S(1)}, u32[]{:S(2)}, u32[]{:S(2)}) collective-permute-start(f32[36,2,256]{2,1,0:T(2,128)S(1)} %get-tuple-element.44), channel_id=1, source_target_pairs={{1,0},{2,1},{3,2},{4,3},{5,4},{6,5},{7,6},{9,8},{10,9},{11,10},{12... | collective-permute-start | bytes 221192 | tf_op jit(solution)/shard_map/ppermute | solution.py:41
  219.5 4.9 %collective-permute-start.32 = (f32[2,32,256]{2,1,0:T(8,128)S(1)}, f32[2,32,256]{2,1,0:T(8,128)S(1)}, u32[]{:S(2)}, u32[]{:S(2)}) collective-permute-start(f32[2,32,256]{2,1,0:T(8,128)S(1)} %get-tuple-element.53), channel_id=1, source_target_pairs={{0,8},{8,16},{16,24},{24,32},{32,40},{40,48},{48,56},{56,64},{64,7... | collective-permute-start | bytes 196616 | tf_op jit(solution)/shard_map/ppermute | solution.py:38
  222.4 9.2 %collective-permute-start.33 = (f32[2,32,256]{2,1,0:T(8,128)S(1)}, f32[2,32,256]{2,1,0:T(8,128)S(1)}, u32[]{:S(2)}, u32[]{:S(2)}) collective-permute-start(f32[2,32,256]{2,1,0:T(8,128)S(1)} %get-tuple-element.54), channel_id=1, source_target_pairs={{8,0},{16,8},{24,16},{32,24},{40,32},{48,40},{56,48},{64,56},{72,6... | collective-permute-start | bytes 196616 | tf_op jit(solution)/shard_map/ppermute | solution.py:41
  231.7 7.3 %collective-permute-start.34 = (f32[36,2,256]{2,1,0:T(2,128)S(1)}, f32[36,2,256]{2,1,0:T(2,128)S(1)}, u32[]{:S(2)}, u32[]{:S(2)}) collective-permute-start(f32[36,2,256]{2,1,0:T(2,128)S(1)} %get-tuple-element.41), channel_id=1, source_target_pairs={{0,1},{1,2},{2,3},{3,4},{4,5},{5,6},{6,7},{8,9},{9,10},{10,11},{11... | collective-permute-start | bytes 221192 | tf_op jit(solution)/shard_map/ppermute | solution.py:38
  236.8 5.1 %collective-permute-start.35 = (f32[36,2,256]{2,1,0:T(2,128)S(1)}, f32[36,2,256]{2,1,0:T(2,128)S(1)}, u32[]{:S(2)}, u32[]{:S(2)}) collective-permute-start(f32[36,2,256]{2,1,0:T(2,128)S(1)} %get-tuple-element.42), channel_id=1, source_target_pairs={{1,0},{2,1},{3,2},{4,3},{5,4},{6,5},{7,6},{9,8},{10,9},{11,10},{12... | collective-permute-start | bytes 221192 | tf_op jit(solution)/shard_map/ppermute | solution.py:41
  244.7 5.2 %collective-permute-start.36 = (f32[2,32,256]{2,1,0:T(8,128)S(1)}, f32[2,32,256]{2,1,0:T(8,128)S(1)}, u32[]{:S(2)}, u32[]{:S(2)}) collective-permute-start(f32[2,32,256]{2,1,0:T(8,128)S(1)} %get-tuple-element.51), channel_id=1, source_target_pairs={{0,8},{8,16},{16,24},{24,32},{32,40},{40,48},{48,56},{56,64},{64,7... | collective-permute-start | bytes 196616 | tf_op jit(solution)/shard_map/ppermute | solution.py:38
  248.0 9.2 %collective-permute-start.37 = (f32[2,32,256]{2,1,0:T(8,128)S(1)}, f32[2,32,256]{2,1,0:T(8,128)S(1)}, u32[]{:S(2)}, u32[]{:S(2)}) collective-permute-start(f32[2,32,256]{2,1,0:T(8,128)S(1)} %get-tuple-element.52), channel_id=1, source_target_pairs={{8,0},{16,8},{24,16},{32,24},{40,32},{48,40},{56,48},{64,56},{72,6... | collective-permute-start | bytes 196616 | tf_op jit(solution)/shard_map/ppermute | solution.py:41
  257.2 6.2 %collective-permute-start.38 = (f32[36,2,256]{2,1,0:T(2,128)S(1)}, f32[36,2,256]{2,1,0:T(2,128)S(1)}, u32[]{:S(2)}, u32[]{:S(2)}) collective-permute-start(f32[36,2,256]{2,1,0:T(2,128)S(1)} %get-tuple-element.39), channel_id=1, source_target_pairs={{0,1},{1,2},{2,3},{3,4},{4,5},{5,6},{6,7},{8,9},{9,10},{10,11},{11... | collective-permute-start | bytes 221192 | tf_op jit(solution)/shard_map/ppermute | solution.py:38
  259.8 5.8 %collective-permute-start.39 = (f32[36,2,256]{2,1,0:T(2,128)S(1)}, f32[36,2,256]{2,1,0:T(2,128)S(1)}, u32[]{:S(2)}, u32[]{:S(2)}) collective-permute-start(f32[36,2,256]{2,1,0:T(2,128)S(1)} %get-tuple-element.40), channel_id=1, source_target_pairs={{1,0},{2,1},{3,2},{4,3},{5,4},{6,5},{7,6},{9,8},{10,9},{11,10},{12... | collective-permute-start | bytes 221192 | tf_op jit(solution)/shard_map/ppermute | solution.py:41
  268.3 4.5 %collective-permute-start.40 = (f32[2,32,256]{2,1,0:T(8,128)S(1)}, f32[2,32,256]{2,1,0:T(8,128)S(1)}, u32[]{:S(2)}, u32[]{:S(2)}) collective-permute-start(f32[2,32,256]{2,1,0:T(8,128)S(1)} %get-tuple-element.49), channel_id=1, source_target_pairs={{0,8},{8,16},{16,24},{24,32},{32,40},{40,48},{48,56},{56,64},{64,7... | collective-permute-start | bytes 196616 | tf_op jit(solution)/shard_map/ppermute | solution.py:38
  270.9 9.2 %collective-permute-start.41 = (f32[2,32,256]{2,1,0:T(8,128)S(1)}, f32[2,32,256]{2,1,0:T(8,128)S(1)}, u32[]{:S(2)}, u32[]{:S(2)}) collective-permute-start(f32[2,32,256]{2,1,0:T(8,128)S(1)} %get-tuple-element.50), channel_id=1, source_target_pairs={{8,0},{16,8},{24,16},{32,24},{40,32},{48,40},{56,48},{64,56},{72,6... | collective-permute-start | bytes 196616 | tf_op jit(solution)/shard_map/ppermute | solution.py:41
  280.2 7.3 %collective-permute-start.42 = (f32[36,2,256]{2,1,0:T(2,128)S(1)}, f32[36,2,256]{2,1,0:T(2,128)S(1)}, u32[]{:S(2)}, u32[]{:S(2)}) collective-permute-start(f32[36,2,256]{2,1,0:T(2,128)S(1)} %get-tuple-element.37), channel_id=1, source_target_pairs={{0,1},{1,2},{2,3},{3,4},{4,5},{5,6},{6,7},{8,9},{9,10},{10,11},{11... | collective-permute-start | bytes 221192 | tf_op jit(solution)/shard_map/ppermute | solution.py:38
  282.7 5.9 %collective-permute-start.43 = (f32[36,2,256]{2,1,0:T(2,128)S(1)}, f32[36,2,256]{2,1,0:T(2,128)S(1)}, u32[]{:S(2)}, u32[]{:S(2)}) collective-permute-start(f32[36,2,256]{2,1,0:T(2,128)S(1)} %get-tuple-element.38), channel_id=1, source_target_pairs={{1,0},{2,1},{3,2},{4,3},{5,4},{6,5},{7,6},{9,8},{10,9},{11,10},{12... | collective-permute-start | bytes 221192 | tf_op jit(solution)/shard_map/ppermute | solution.py:41
  301.2 23.1 %copy-start.1 = (f32[64,64,256]{2,1,0:T(8,128)S(1)}, f32[64,64,256]{2,1,0:T(8,128)}, u32[]{:S(2)}) copy-start(f32[64,64,256]{2,1,0:T(8,128)} %param.5) | copy-start | bytes 12582916
  301.2 23.1 %copy-start.3 = (f32[64,64,256]{2,1,0:T(8,128)S(1)}, f32[64,64,256]{2,1,0:T(8,128)}, u32[]{:S(2)}) copy-start(f32[64,64,256]{2,1,0:T(8,128)} %param.3) | copy-start | bytes 12582916
  305.7 11.3 %collective-permute-start.46 = (f32[64,1,256]{2,1,0:T(1,128)S(1)}, f32[64,1,256]{2,1,0:T(1,128)S(1)}, u32[]{:S(2)}, u32[]{:S(2)}) collective-permute-start(f32[64,1,256]{2,1,0:T(1,128)S(1)} %get-tuple-element.13), channel_id=1, source_target_pairs={{0,1},{1,2},{2,3},{3,4},{4,5},{5,6},{6,7},{8,9},{9,10},{10,11},{11... | collective-permute-start | bytes 196616 | tf_op jit(solution)/shard_map/ppermute | solution.py:19
  307.9 9.2 %collective-permute-start.47 = (f32[64,1,256]{2,1,0:T(1,128)S(1)}, f32[64,1,256]{2,1,0:T(1,128)S(1)}, u32[]{:S(2)}, u32[]{:S(2)}) collective-permute-start(f32[64,1,256]{2,1,0:T(1,128)S(1)} %get-tuple-element.14), channel_id=1, source_target_pairs={{1,0},{2,1},{3,2},{4,3},{5,4},{6,5},{7,6},{9,8},{10,9},{11,10},{12... | collective-permute-start | bytes 196616 | tf_op jit(solution)/shard_map/ppermute | solution.py:19
  312.4 4.7 %collective-permute-start.44 = (f32[1,64,256]{2,1,0:T(8,128)S(1)}, f32[1,64,256]{2,1,0:T(8,128)S(1)}, u32[]{:S(2)}, u32[]{:S(2)}) collective-permute-start(f32[1,64,256]{2,1,0:T(8,128)S(1)} %get-tuple-element.15), channel_id=1, source_target_pairs={{0,8},{8,16},{16,24},{24,32},{32,40},{40,48},{48,56},{56,64},{64,7... | collective-permute-start | bytes 196616 | tf_op jit(solution)/shard_map/ppermute | solution.py:19
  315.1 9.2 %collective-permute-start.45 = (f32[1,64,256]{2,1,0:T(8,128)S(1)}, f32[1,64,256]{2,1,0:T(8,128)S(1)}, u32[]{:S(2)}, u32[]{:S(2)}) collective-permute-start(f32[1,64,256]{2,1,0:T(8,128)S(1)} %get-tuple-element.16), channel_id=1, source_target_pairs={{8,0},{16,8},{24,16},{32,24},{40,32},{48,40},{56,48},{64,56},{72,6... | collective-permute-start | bytes 196616 | tf_op jit(solution)/shard_map/ppermute | solution.py:19
  330.1 10.6 %collective-permute-start.50 = (f32[64,1,256]{2,1,0:T(1,128)S(1)}, f32[64,1,256]{2,1,0:T(1,128)S(1)}, u32[]{:S(2)}, u32[]{:S(2)}) collective-permute-start(f32[64,1,256]{2,1,0:T(1,128)S(1)} %get-tuple-element.9), channel_id=1, source_target_pairs={{0,1},{1,2},{2,3},{3,4},{4,5},{5,6},{6,7},{8,9},{9,10},{10,11},{11... | collective-permute-start | bytes 196616 | tf_op jit(solution)/shard_map/ppermute | solution.py:19
  332.0 8.6 %collective-permute-start.51 = (f32[64,1,256]{2,1,0:T(1,128)S(1)}, f32[64,1,256]{2,1,0:T(1,128)S(1)}, u32[]{:S(2)}, u32[]{:S(2)}) collective-permute-start(f32[64,1,256]{2,1,0:T(1,128)S(1)} %get-tuple-element.10), channel_id=1, source_target_pairs={{1,0},{2,1},{3,2},{4,3},{5,4},{6,5},{7,6},{9,8},{10,9},{11,10},{12... | collective-permute-start | bytes 196616 | tf_op jit(solution)/shard_map/ppermute | solution.py:19
  336.3 4.4 %collective-permute-start.48 = (f32[1,64,256]{2,1,0:T(8,128)S(1)}, f32[1,64,256]{2,1,0:T(8,128)S(1)}, u32[]{:S(2)}, u32[]{:S(2)}) collective-permute-start(f32[1,64,256]{2,1,0:T(8,128)S(1)} %get-tuple-element.11), channel_id=1, source_target_pairs={{0,8},{8,16},{16,24},{24,32},{32,40},{40,48},{48,56},{56,64},{64,7... | collective-permute-start | bytes 196616 | tf_op jit(solution)/shard_map/ppermute | solution.py:19
  338.8 9.2 %collective-permute-start.49 = (f32[1,64,256]{2,1,0:T(8,128)S(1)}, f32[1,64,256]{2,1,0:T(8,128)S(1)}, u32[]{:S(2)}, u32[]{:S(2)}) collective-permute-start(f32[1,64,256]{2,1,0:T(8,128)S(1)} %get-tuple-element.12), channel_id=1, source_target_pairs={{8,0},{16,8},{24,16},{32,24},{40,32},{48,40},{56,48},{64,56},{72,6... | collective-permute-start | bytes 196616 | tf_op jit(solution)/shard_map/ppermute | solution.py:19
  353.7 24.4 %copy-start.5 = (f32[64,64,256]{2,1,0:T(8,128)}, f32[64,64,256]{2,1,0:T(8,128)S(1)}, u32[]{:S(2)}) copy-start(f32[64,64,256]{2,1,0:T(8,128)S(1)} %fusion.13) | copy-start | bytes 12582916
  353.8 10.6 %collective-permute-start.54 = (f32[64,1,256]{2,1,0:T(1,128)S(1)}, f32[64,1,256]{2,1,0:T(1,128)S(1)}, u32[]{:S(2)}, u32[]{:S(2)}) collective-permute-start(f32[64,1,256]{2,1,0:T(1,128)S(1)} %get-tuple-element.5), channel_id=1, source_target_pairs={{0,1},{1,2},{2,3},{3,4},{4,5},{5,6},{6,7},{8,9},{9,10},{10,11},{11... | collective-permute-start | bytes 196616 | tf_op jit(solution)/shard_map/ppermute | solution.py:19
  355.7 8.6 %collective-permute-start.55 = (f32[64,1,256]{2,1,0:T(1,128)S(1)}, f32[64,1,256]{2,1,0:T(1,128)S(1)}, u32[]{:S(2)}, u32[]{:S(2)}) collective-permute-start(f32[64,1,256]{2,1,0:T(1,128)S(1)} %get-tuple-element.6), channel_id=1, source_target_pairs={{1,0},{2,1},{3,2},{4,3},{5,4},{6,5},{7,6},{9,8},{10,9},{11,10},{12... | collective-permute-start | bytes 196616 | tf_op jit(solution)/shard_map/ppermute | solution.py:19
  360.0 4.4 %collective-permute-start.52 = (f32[1,64,256]{2,1,0:T(8,128)S(1)}, f32[1,64,256]{2,1,0:T(8,128)S(1)}, u32[]{:S(2)}, u32[]{:S(2)}) collective-permute-start(f32[1,64,256]{2,1,0:T(8,128)S(1)} %get-tuple-element.7), channel_id=1, source_target_pairs={{0,8},{8,16},{16,24},{24,32},{32,40},{40,48},{48,56},{56,64},{64,7... | collective-permute-start | bytes 196616 | tf_op jit(solution)/shard_map/ppermute | solution.py:19
  362.4 9.2 %collective-permute-start.53 = (f32[1,64,256]{2,1,0:T(8,128)S(1)}, f32[1,64,256]{2,1,0:T(8,128)S(1)}, u32[]{:S(2)}, u32[]{:S(2)}) collective-permute-start(f32[1,64,256]{2,1,0:T(8,128)S(1)} %get-tuple-element.8), channel_id=1, source_target_pairs={{8,0},{16,8},{24,16},{32,24},{40,32},{48,40},{56,48},{64,56},{72,6... | collective-permute-start | bytes 196616 | tf_op jit(solution)/shard_map/ppermute | solution.py:19
where the time goes:
time: 385 us; the launch traced here: 378 us
  starting transfers between devices  174 us (45%)
  waiting for transfers between devices  87.4 us (23%)
  other arithmetic  83.8 us (22%)
  local copies, waits for them, and re-layouts  31.1 us (8%)
    ppermute x14, starting transfers between devices, padded_2(): lax.ppermute(lax.slice_in_dim(block, block.shape[dim] - width, None, axis...  56.6 us
    ppermute x14, waiting for transfers between devices, padded_2(): lax.ppermute(lax.slice_in_dim(block, 0, width, axis=dim), axis, backward)  51 us
    ppermute x14, starting transfers between devices, extended(): lax.ppermute(leading, axis, [(b, a) for a, b in up])  42.2 us
    ppermute x14, starting transfers between devices, extended(): lax.ppermute(last, axis, up)  37.8 us
    ppermute x14, starting transfers between devices, padded_2(): lax.ppermute(lax.slice_in_dim(block, 0, width, axis=dim), axis, backward)  37.3 us
    ppermute x14, waiting for transfers between devices, extended(): lax.ppermute(leading, axis, [(b, a) for a, b in up])  36.1 us
    add x11, other arithmetic, smooth_step(): values + 0.8 * (load + cross_sum(padded) - (4.0 + mass_here) * values) /...  32.9 us
    sub x1, other arithmetic, body(): load_terms + cross_sum(extended(values, (('band', 0), ('lane', 1)), 1, Fa...  13.6 us
  transfers between devices with their start and end apart: 56, of which 18 were waited for; matrix products, arithmetic and copies ran while one was open for 4% of the time, Pallas kernels for 0%

commit v1 on v0

v1 whole, which is shorter than its diff:
```python
import functools

import jax
import jax.numpy as jnp
import numpy as np
from jax import lax
from jax.experimental import pallas as pl
from jax.experimental.pallas import tpu as pltpu
from jax.sharding import PartitionSpec as P

BEFORE = 3
INNER = 13
LANES = 128
GROUPS = 2
DEPTHS = (5, 4, 4)
PAD = 5
WEIGHT = np.float32(0.8)
KEEP = np.float32(1.0) - WEIGHT
MESH = pl.DeviceIdType.MESH

OFFSETS = ((-1, 0), (1, 0), (0, -1), (0, 1), (-1, -1), (-1, 1), (1, -1), (1, 1))
OPPOSITE = (1, 0, 3, 2, 7, 6, 5, 4)


def kernel(
    height, width, load_hbm, start_hbm, mass_hbm, sol_hbm, rem_hbm,
    fine, load, mass, coef, column_out, column_in, coarse, coarse_load, coarse_coef,
    edge_out, edge_in, corner_out, corner_in, temp,
    load_sem, out_sem, fine_send, fine_recv, coarse_send, coarse_recv,
):
    h, w = height // 2, width // 2
    pitch, coarse_pitch = width + 8, w + 16
    cells = height * width
    part = min(32, width)
    band, lane = lax.axis_index("band"), lax.axis_index("lane")
    bands, lanes = lax.axis_size("band"), lax.axis_size("lane")
    inside = {-1: (band > 0, lane > 0), 1: (band < bands - 1, lane < lanes - 1)}
    has = []
    for dy, dx in OFFSETS:
        if dx == 0:
            has.append(inside[dy][0])
        elif dy == 0:
            has.append(inside[dx][1])
        else:
            has.append(jnp.logical_and(inside[dy][0], inside[dx][1]))

    def neighbour(side):
        dy, dx = OFFSETS[side]
        return (band + dy, lane + dx)

    def at(y):
        return (y + 1) * pitch + 8

    def coarse_at(y):
        return (y + PAD) * coarse_pitch + 8

    def group_lanes(g):
        return pl.ds(g * LANES, LANES)

    def start_inputs():
        for g in range(GROUPS):
            target = fine.at[g, 0]

            @pl.loop(0, height)
            def _(y):
                pltpu.make_async_copy(
                    start_hbm.at[pl.ds(pl.multiple_of(y * width, 8), width), group_lanes(g)],
                    target.at[pl.ds(pl.multiple_of(at(y), 8), width), :],
                    load_sem.at[0, g],
                ).start()

        for g in range(GROUPS):
            pltpu.make_async_copy(mass_hbm.at[:, group_lanes(g)], mass.at[g], load_sem.at[1, g]).start()
            pltpu.make_async_copy(load_hbm.at[:, group_lanes(g)], load.at[g], load_sem.at[2, g]).start()

    def wait_input(which, g):
        source, target = ((start_hbm, coef), (mass_hbm, mass), (load_hbm, load))[which]
        pltpu.make_async_copy(source.at[:, group_lanes(g)], target.at[g], load_sem.at[which, g]).wait()

    def clear():
        zero8 = jnp.zeros((8, LANES), jnp.float32)
        for g in range(GROUPS):
            for b in range(2):
                ref = fine.at[g, b]
                ref[pl.ds(0, pitch), :] = jnp.zeros((pitch, LANES), jnp.float32)
                ref[pl.ds((height + 1) * pitch, pitch + 8), :] = jnp.zeros((pitch + 8, LANES), jnp.float32)

                @pl.loop(0, height // 8)
                def _(i):
                    for r in range(8):
                        ref[pl.ds(pl.multiple_of((i * 8 + r + 1) * pitch, 8), 8), :] = zero8

            rows = (h + 2 * PAD) * coarse_pitch // (h + 2 * PAD)

            @pl.loop(0, h + 2 * PAD)
            def _(y):
                for ref in (coarse.at[g, 1], coarse_load.at[g], coarse_coef.at[g]):
                    ref[pl.ds(pl.multiple_of(y * rows, 8), rows), :] = jnp.zeros((rows, LANES), jnp.float32)

    def enter():
        barrier = pltpu.get_barrier_semaphore()
        count = jnp.int32(0)
        for side in range(8):
            count = count + has[side].astype(jnp.int32)

            @pl.when(has[side])
            def _():
                pl.semaphore_signal(barrier, inc=1, device_id=neighbour(side), device_id_type=MESH)

        pl.semaphore_wait(barrier, count)

    def fine_copy(g, b, side):
        if side < 2:
            source = fine.at[g, b, pl.ds(at(0) if side == 0 else at(height - 1), width), :]
            target = fine.at[g, b, pl.ds(at(height) if side == 0 else at(-1), width), :]
        else:
            source = column_out.at[g, b, side - 2]
            target = column_in.at[g, b, OPPOSITE[side] - 2]
        return pltpu.make_async_remote_copy(
            src_ref=source, dst_ref=target,
            send_sem=fine_send.at[g, b, side], recv_sem=fine_recv.at[g, b, OPPOSITE[side]],
            device_id=neighbour(side), device_id_type=MESH,
        )

    def fine_arrival(g, b, side):
        if side < 2:
            target = fine.at[g, b, pl.ds(at(-1) if side == 0 else at(height), width), :]
        else:
            target = column_in.at[g, b, side - 2]
        return pltpu.make_async_remote_copy(
            src_ref=target, dst_ref=target,
            send_sem=fine_send.at[g, b, OPPOSITE[side]], recv_sem=fine_recv.at[g, b, side],
            device_id=neighbour(side), device_id_type=MESH,
        )

    def send_fine(g, b):
        ref = fine.at[g, b]
        for side, x in ((2, 0), (3, width - 1)):
            out = column_out.at[g, b, side - 2]
            for i in range(height // 8):
                out[pl.ds(8 * i, 8), :] = ref[pl.ds(at(8 * i) + x, 8, stride=pitch), :]
        for side in range(4):
            pl.when(has[side])(lambda side=side: fine_copy(g, b, side).start())

    def sent_fine(g, b):
        for side in range(4):
            pl.when(has[side])(lambda side=side: fine_copy(g, b, side).wait_send())

    def receive_fine(g, b):
        ref = fine.at[g, b]
        for side in range(4):
            pl.when(has[side])(lambda side=side: fine_arrival(g, b, side).wait_recv())
        for side, x in ((2, -1), (3, width)):

            @pl.when(has[side])
            def _():
                column = column_in.at[g, b, side - 2]
                for i in range(height // 8):
                    ref[pl.ds(at(8 * i) + x, 8, stride=pitch), :] = column[pl.ds(8 * i, 8), :]

    def fine_loop(g, b, finish, rows=8):
        ref = fine.at[g, b]

        @pl.loop(0, height // rows)
        def _(i):
            top = i * rows
            for p in range(width // part):
                centre = [
                    ref[pl.ds(pl.multiple_of(at(top + r - 1) + p * part, 8), part), :]
                    for r in range(rows + 2)
                ]
                for r in range(rows):
                    here = at(top + r) + p * part
                    around = (centre[r] + centre[r + 2]) + (
                        ref[pl.ds(here - 1, part), :] + ref[pl.ds(here + 1, part), :]
                    )
                    flat = pl.multiple_of((top + r) * width + p * part, 8)
                    finish(top, r, p, pl.multiple_of(here, 8), flat, centre[r + 1], around)

    def sweep_fine(g, b):
        out = fine.at[g, 1 - b]

        def finish(top, r, p, here, flat, centre, around):
            total = load[g, pl.ds(flat, part), :] + around
            out[pl.ds(here, part), :] = KEEP * centre + coef[g, pl.ds(flat, part), :] * total

        fine_loop(g, b, finish)

    def defect(g, flat, centre, around):
        return (load[g, pl.ds(flat, part), :] + around) - (4.0 + mass[g, pl.ds(flat, part), :]) * centre

    def halve(ref, slot, pair):
        scratch = ref.at[slot]
        scratch[...] = pair
        return scratch[pl.ds(0, part // 2, stride=2), :] + scratch[pl.ds(1, part // 2, stride=2), :]

    def coarsen_mass(g):
        rows = 4

        @pl.loop(0, height // rows)
        def _(i):
            for p in range(width // part):
                for r in range(0, rows, 2):
                    pair = []
                    for s in range(2):
                        flat = pl.multiple_of((i * rows + r + s) * width + p * part, 8)
                        here = mass[g, pl.ds(flat, part), :]
                        coef[g, pl.ds(flat, part), :] = WEIGHT / (4.0 + here)
                        pair.append(here)
                    summed = 0.5 * halve(temp, p * (rows // 2) + r // 2, pair[0] + pair[1])
                    place = coarse_at(i * (rows // 2) + r // 2) + p * (part // 2)
                    coarse_coef[g, pl.ds(pl.multiple_of(place, 8), part // 2), :] = WEIGHT / (4.0 + summed)

    def coarsen_defect(g, b):
        held = {}

        def finish(top, r, p, here, flat, centre, around):
            value = defect(g, flat, centre, around)
            if r % 2 == 0:
                held[p] = value
            else:
                summed = 0.5 * halve(temp, p * 4 + r // 2, held[p] + value)
                place = coarse_at(top // 2 + r // 2) + p * (part // 2)
                coarse_load[g, pl.ds(pl.multiple_of(place, 8), part // 2), :] = summed

        fine_loop(g, b, finish)

    def remain(g, b):
        def finish(top, r, p, here, flat, centre, around):
            coef[g, pl.ds(flat, part), :] = defect(g, flat, centre, around)

        fine_loop(g, b, finish)

    def blocks(side, depth):
        corner = depth - 1
        dy, dx = OFFSETS[side]
        if dx == 0:
            return (depth, w, 0 if dy < 0 else h - depth, 0, -depth if dy < 0 else h, 0)
        if dy == 0:
            return (h, depth, 0, 0 if dx < 0 else w - depth, 0, -depth if dx < 0 else w)
        return (
            corner, corner, 0 if dy < 0 else h - corner, 0 if dx < 0 else w - corner,
            -corner if dy < 0 else h, -corner if dx < 0 else w,
        )

    def buffers(g, e, side, depth):
        rows, columns = blocks(side, depth)[:2]
        if side < 4:
            return (
                edge_out.at[g, e, side, pl.ds(0, rows * columns), :],
                edge_in.at[g, e, side, pl.ds(0, rows * columns), :],
                edge_in.at[g, e, OPPOSITE[side], pl.ds(0, rows * columns), :],
            )
        return (
            corner_out.at[g, e, side - 4, pl.ds(0, rows * columns), :],
            corner_in.at[g, e, side - 4, pl.ds(0, rows * columns), :],
            corner_in.at[g, e, OPPOSITE[side] - 4, pl.ds(0, rows * columns), :],
        )

    def move(rows, columns, source, source_at, target, target_at):
        step = 8
        if rows % step == 0:

            @pl.loop(0, rows // step)
            def _(i):
                for r in range(step):
                    y = i * step + r
                    target[pl.ds(target_at(y), columns), :] = source[pl.ds(source_at(y), columns), :]
        else:
            for y in range(rows):
                target[pl.ds(target_at(y), columns), :] = source[pl.ds(source_at(y), columns), :]

    def sides_of(depth):
        return range(8 if depth > 1 else 4)

    def coarse_copy(g, e, side, depth):
        out, _, there = buffers(g, e, side, depth)
        return pltpu.make_async_remote_copy(
            src_ref=out, dst_ref=there,
            send_sem=coarse_send.at[g, e, side], recv_sem=coarse_recv.at[g, e, OPPOSITE[side]],
            device_id=neighbour(side), device_id_type=MESH,
        )

    def coarse_arrival(g, e, side, depth):
        _, here, _ = buffers(g, e, side, depth)
        return pltpu.make_async_remote_copy(
            src_ref=here, dst_ref=here,
            send_sem=coarse_send.at[g, e, OPPOSITE[side]], recv_sem=coarse_recv.at[g, e, side],
            device_id=neighbour(side), device_id_type=MESH,
        )

    def send_coarse(g, e, depth, ref):
        for side in sides_of(depth):
            rows, columns, y0, x0, _, _ = blocks(side, depth)
            out = edge_out.at[g, e, side] if side < 4 else corner_out.at[g, e, side - 4]
            move(rows, columns, ref, lambda y: coarse_at(y0 + y) + x0, out, lambda y: y * columns)
        for side in sides_of(depth):
            pl.when(has[side])(lambda side=side: coarse_copy(g, e, side, depth).start())

    def receive_coarse(g, e, depth, ref):
        for side in sides_of(depth):

            @pl.when(has[side])
            def _():
                coarse_arrival(g, e, side, depth).wait_recv()
                rows, columns, _, _, y1, x1 = blocks(side, depth)
                held = edge_in.at[g, e, side] if side < 4 else corner_in.at[g, e, side - 4]
                move(rows, columns, held, lambda y: y * columns, ref, lambda y: coarse_at(y1 + y) + x1)

    def sent_coarse(g, e, depth):
        for side in sides_of(depth):
            pl.when(has[side])(lambda side=side: coarse_copy(g, e, side, depth).wait_send())

    def first_coarse(g):
        out = coarse.at[g, 0]

        @pl.loop(0, h + 2 * PAD)
        def _(y):
            here = pl.ds(pl.multiple_of(y * coarse_pitch, 8), coarse_pitch)
            out[here, :] = coarse_coef[g, here, :] * coarse_load[g, here, :]

    def sweep_coarse(g, b, valid):
        ref, out = coarse.at[g, b], coarse.at[g, 1 - b]
        rim = (valid + 1) // 2 * 2
        span, left = (w + 8, -4) if valid else (w, 0)
        rows = 4

        @pl.loop(0, (h + 2 * rim) // rows)
        def _(i):
            top = i * rows - rim
            centre = [ref[pl.ds(coarse_at(top + r - 1) + left, span), :] for r in range(rows + 2)]
            for r in range(rows):
                here = coarse_at(top + r) + left
                around = (centre[r] + centre[r + 2]) + (
                    ref[pl.ds(here - 1, span), :] + ref[pl.ds(here + 1, span), :]
                )
                total = coarse_load[g, pl.ds(here, span), :] + around
                out[pl.ds(here, span), :] = KEEP * centre[r + 1] + coarse_coef[g, pl.ds(here, span), :] * total

    def correct(g, b, c):
        ref, values = fine.at[g, b], coarse.at[g, c]

        def spread(slot, value):
            scratch = temp.at[slot]
            scratch[pl.ds(0, part // 2, stride=2), :] = value
            scratch[pl.ds(1, part // 2, stride=2), :] = value
            return scratch[...]

        def add(y, wide, p):
            here = pl.ds(pl.multiple_of(at(y) + p * part, 8), part)
            ref[here, :] = ref[here, :] + wide

        rows = 4

        @pl.loop(0, h // rows)
        def _(i):
            for r in range(rows):
                for p in range(width // part):
                    place = coarse_at(i * rows + r) + p * (part // 2)
                    wide = spread(r * 2 + p, values[pl.ds(pl.multiple_of(place, 8), part // 2), :])
                    for s in range(2):
                        add((i * rows + r) * 2 + s, wide, p)

        for side, y in ((0, -1), (1, height)):
            for p in range(width // part):
                place = coarse_at(-1 if y < 0 else h) + p * (part // 2)
                add(y, spread(side * 2 + p, values[pl.ds(place, part // 2), :]), p)
        for side, x in ((2, -1), (3, width)):
            for p in range(height // part):
                place = coarse_at(p * (part // 2)) + (-1 if x < 0 else w)
                wide = spread(side * 2 + p, values[pl.ds(place, part // 2, stride=coarse_pitch), :])
                for i in range(part // 8):
                    here = pl.ds(at(p * part + 8 * i) + x, 8, stride=pitch)
                    ref[here, :] = ref[here, :] + wide[8 * i : 8 * i + 8]

    def write_solution(g, b):
        ref = fine.at[g, b]

        @pl.loop(0, height)
        def _(y):
            pltpu.make_async_copy(
                ref.at[pl.ds(pl.multiple_of(at(y), 8), width), :],
                sol_hbm.at[pl.ds(pl.multiple_of(y * width, 8), width), group_lanes(g)],
                out_sem.at[0, g],
            ).start()

    def remaining_copy(g):
        return pltpu.make_async_copy(coef.at[g], rem_hbm.at[:, group_lanes(g)], out_sem.at[1, g])

    both = range(GROUPS)
    start_inputs()
    clear()
    enter()
    for g in both:
        wait_input(0, g)
        send_fine(g, 0)
    for g in both:
        wait_input(1, g)
        coarsen_mass(g)
        wait_input(2, g)
    now = 0
    for sweep in range(BEFORE):
        for g in both:
            receive_fine(g, now)
            if sweep >= 1:
                sent_fine(g, 1 - now)
            sweep_fine(g, now)
            send_fine(g, 1 - now)
            if sweep < GROUPS:
                send_coarse(sweep, 0, DEPTHS[0], coarse_coef.at[sweep]) if g == GROUPS - 1 else None
        now = 1 - now
    for g in both:
        receive_fine(g, now)
        coarsen_defect(g, now)
        send_coarse(g, 1, DEPTHS[0], coarse_load.at[g])
    for g in both:
        receive_coarse(g, 0, DEPTHS[0], coarse_coef.at[g])
    inner, valid, c = 1, DEPTHS[0], 0
    for e, depth in enumerate(DEPTHS):
        last = e == len(DEPTHS) - 1
        count = depth - 1 if last else depth
        for g in both:
            b = c
            if e == 0:
                receive_coarse(g, 1, depth, coarse_load.at[g])
                first_coarse(g)
            else:
                receive_coarse(g, 1 + e, depth, coarse.at[g, b])
            for i in range(count):
                sweep_coarse(g, b, depth - 1 - i)
                b = 1 - b
            if not last:
                send_coarse(g, 2 + e, DEPTHS[e + 1], coarse.at[g, b])
            else:
                sent_fine(g, now)
                correct(g, now, b)
                sent_fine(g, 1 - now)
                sweep_fine(g, now)
                send_fine(g, 1 - now)
        c = (c + count) % 2
        inner += count
    assert inner == INNER
    now = 1 - now
    for g in both:
        receive_fine(g, now)
        sweep_fine(g, now)
        send_fine(g, 1 - now)
        write_solution(g, 1 - now)
    now = 1 - now
    for g in both:
        receive_fine(g, now)
        remain(g, now)
        remaining_copy(g).start()
    for g in both:
        for b in range(2):
            sent_fine(g, b)
        for e in range(len(DEPTHS) + 1):
            sent_coarse(g, e, DEPTHS[max(e - 1, 0)])
        pltpu.make_async_copy(coef.at[g], sol_hbm.at[:, group_lanes(g)], out_sem.at[0, g]).wait()
        remaining_copy(g).wait()


def body(load_terms, start_values, reaction_rate):
    height, width, layers = load_terms.shape
    h, w = height // 2, width // 2
    flat = (height * width, layers)
    fine_rows = (height + 2) * (width + 8) + 8
    coarse_rows = (h + 2 * PAD) * (w + 16)
    exchanges = len(DEPTHS) + 1
    edge = max(DEPTHS) * max(h, w)
    corner = -(-((max(DEPTHS) - 1) ** 2) // 8) * 8
    f32 = jnp.float32
    any_space = pl.BlockSpec(memory_space=pl.ANY)
    results = pl.pallas_call(
        functools.partial(kernel, height, width),
        out_shape=[jax.ShapeDtypeStruct(flat, f32)] * 2,
        in_specs=[any_space] * 3,
        out_specs=[any_space] * 2,
        scratch_shapes=[
            pltpu.VMEM((GROUPS, 2, fine_rows, LANES), f32),
            pltpu.VMEM((GROUPS, height * width, LANES), f32),
            pltpu.VMEM((GROUPS, height * width, LANES), f32),
            pltpu.VMEM((GROUPS, height * width, LANES), f32),
            pltpu.VMEM((GROUPS, 2, 2, height, LANES), f32),
            pltpu.VMEM((GROUPS, 2, 2, height, LANES), f32),
            pltpu.VMEM((GROUPS, 2, coarse_rows, LANES), f32),
            pltpu.VMEM((GROUPS, coarse_rows, LANES), f32),
            pltpu.VMEM((GROUPS, coarse_rows, LANES), f32),
            pltpu.VMEM((GROUPS, exchanges, 4, edge, LANES), f32),
            pltpu.VMEM((GROUPS, exchanges, 4, edge, LANES), f32),
            pltpu.VMEM((GROUPS, exchanges, 4, corner, LANES), f32),
            pltpu.VMEM((GROUPS, exchanges, 4, corner, LANES), f32),
            pltpu.VMEM((8, min(32, width), LANES), f32),
            pltpu.SemaphoreType.DMA((3, GROUPS)),
            pltpu.SemaphoreType.DMA((2, GROUPS)),
            pltpu.SemaphoreType.DMA((GROUPS, 2, 4)),
            pltpu.SemaphoreType.DMA((GROUPS, 2, 4)),
            pltpu.SemaphoreType.DMA((GROUPS, exchanges, 8)),
            pltpu.SemaphoreType.DMA((GROUPS, exchanges, 8)),
        ],
        compiler_params=pltpu.CompilerParams(
            collective_id=0, has_side_effects=True, vmem_limit_bytes=50 * 1024 * 1024
        ),
    )(load_terms.reshape(flat), start_values.reshape(flat), reaction_rate.reshape(flat))
    return tuple(result.reshape(height, width, layers) for result in results)


def solution(mesh):
    spec = P("band", "lane", None)
    return jax.shard_map(
        body, mesh=mesh, in_specs=(spec, spec, spec), out_specs=(spec, spec), check_vma=False
    )
```

time: 385 us -> 91.9 us (0.24)
  the two profiles are of different devices: /device:TPU:109 before, /device:TPU:57 now
where the time goes in v1:
time: 91.9 us; the launch traced here: 91.7 us
  Pallas kernels  84.2 us (92%)
  local copies, waits for them, and re-layouts  6.87 us (7%)
    pallas_call x1, Pallas kernels, body(): pl.pallas_call(functools.partial(kernel, height, width), out_shape=[jax.S...  84.2 us
    unnamed x4, local copies, waits for them, and re-layouts  6.87 us

profile of v1, /device:TPU:57, one launch (start us, length us, event | category | flops | bytes accessed | tf_op | source)
XLA Modules:
  0.0 91.7 jit_solution(18060867928002945455)
XLA Ops:
  0.6 84.2 %shard_map.50 = (f32[4096,256]{1,0:T(8,128)}, f32[4096,256]{1,0:T(8,128)}) custom-call(f32[4096,256]{1,0:T(8,128)} %bitcast.5, f32[4096,256]{1,0:T(8,128)} %bitcast.6, f32[4096,256]{1,0:T(8,128)} %bitcast.7), custom_call_target="tpu_custom_call" | custom-call | tf_op jit(solution)/shard_map/pallas_call | solution.py:474
  84.8 0.0 copy-start
  84.8 4.8 %copy.7 = f32[64,64,256]{2,1,0:T(8,128)} copy(f32[64,64,256]{2,1,0:T(8,128)} %bitcast.9) | data formatting | bytes 8388608
  89.7 0.0 copy-done
  89.7 2.0 %copy.8 = f32[64,64,256]{2,1,0:T(8,128)} copy(f32[64,64,256]{2,1,0:T(8,128)S(1)} %bitcast.8) | data formatting | bytes 8388608
Async XLA Ops:
  84.8 4.9 %copy-start = (f32[4096,256]{1,0:T(8,128)S(1)}, f32[4096,256]{1,0:T(8,128)}, u32[]{:S(2)}) copy-start(f32[4096,256]{1,0:T(8,128)} %get-tuple-element.5) | copy-start | bytes 12582916

commit v2 on v1

--- a/solution.py
+++ b/solution.py
@@ -12,7 +12,7 @@
 INNER = 13
 LANES = 128
 GROUPS = 2
-DEPTHS = (5, 4, 4)
+DEPTHS = (3, 3, 3, 4)
 PAD = 5
 WEIGHT = np.float32(0.8)
 KEEP = np.float32(1.0) - WEIGHT
@@ -23,10 +23,10 @@
 
 
 def kernel(
-    height, width, load_hbm, start_hbm, mass_hbm, sol_hbm, rem_hbm,
-    fine, load, mass, coef, column_out, column_in, coarse, coarse_load, coarse_coef,
+    height, width, load_hbm, start_hbm, mass_hbm, final, load, mass,
+    fine, coef, row_in, column_out, column_in, coarse, coarse_load, coarse_coef,
     edge_out, edge_in, corner_out, corner_in, temp,
-    load_sem, out_sem, fine_send, fine_recv, coarse_send, coarse_recv,
+    load_sem, fine_send, fine_recv, coarse_send, coarse_recv,
 ):
     h, w = height // 2, width // 2
     pitch, coarse_pitch = width + 8, w + 16
@@ -57,45 +57,54 @@
     def group_lanes(g):
         return pl.ds(g * LANES, LANES)
 
-    def start_inputs():
-        for g in range(GROUPS):
-            target = fine.at[g, 0]
-
-            @pl.loop(0, height)
-            def _(y):
-                pltpu.make_async_copy(
-                    start_hbm.at[pl.ds(pl.multiple_of(y * width, 8), width), group_lanes(g)],
-                    target.at[pl.ds(pl.multiple_of(at(y), 8), width), :],
-                    load_sem.at[0, g],
-                ).start()
-
-        for g in range(GROUPS):
-            pltpu.make_async_copy(mass_hbm.at[:, group_lanes(g)], mass.at[g], load_sem.at[1, g]).start()
-            pltpu.make_async_copy(load_hbm.at[:, group_lanes(g)], load.at[g], load_sem.at[2, g]).start()
+    def start_values(g):
+        target = fine.at[g, 0]
+
+        @pl.loop(0, height)
+        def _(y):
+            pltpu.make_async_copy(
+                start_hbm.at[pl.ds(pl.multiple_of(y * width, 8), width), group_lanes(g)],
+                target.at[pl.ds(pl.multiple_of(at(y), 8), width), :],
+                load_sem.at[0, g],
+            ).start()
+
+    def start_terms(g):
+        pltpu.make_async_copy(mass_hbm.at[:, group_lanes(g)], mass.at[g], load_sem.at[1, g]).start()
+        pltpu.make_async_copy(load_hbm.at[:, group_lanes(g)], load.at[g], load_sem.at[2, g]).start()
 
     def wait_input(which, g):
         source, target = ((start_hbm, coef), (mass_hbm, mass), (load_hbm, load))[which]
         pltpu.make_async_copy(source.at[:, group_lanes(g)], target.at[g], load_sem.at[which, g]).wait()
 
-    def clear():
-        zero8 = jnp.zeros((8, LANES), jnp.float32)
+    def clear_rows():
         for g in range(GROUPS):
             for b in range(2):
-                ref = fine.at[g, b]
-                ref[pl.ds(0, pitch), :] = jnp.zeros((pitch, LANES), jnp.float32)
-                ref[pl.ds((height + 1) * pitch, pitch + 8), :] = jnp.zeros((pitch + 8, LANES), jnp.float32)
-
-                @pl.loop(0, height // 8)
-                def _(i):
-                    for r in range(8):
-                        ref[pl.ds(pl.multiple_of((i * 8 + r + 1) * pitch, 8), 8), :] = zero8
-
-            rows = (h + 2 * PAD) * coarse_pitch // (h + 2 * PAD)
-
-            @pl.loop(0, h + 2 * PAD)
-            def _(y):
-                for ref in (coarse.at[g, 1], coarse_load.at[g], coarse_coef.at[g]):
-                    ref[pl.ds(pl.multiple_of(y * rows, 8), rows), :] = jnp.zeros((rows, LANES), jnp.float32)
+                fine[g, b, pl.ds(at(-1), width), :] = jnp.zeros((width, LANES), jnp.float32)
+                fine[g, b, pl.ds(at(height), width), :] = jnp.zeros((width, LANES), jnp.float32)
+
+    def clear_rest(g):
+        zero8 = jnp.zeros((8, LANES), jnp.float32)
+        step = 8
+
+        @pl.loop(0, height // step)
+        def _(i):
+            for r in range(step):
+                here = pl.ds(pl.multiple_of((i * step + r + 1) * pitch, 8), 8)
+                fine[g, 0, here, :] = zero8
+                fine[g, 1, here, :] = zero8
+                final[g, here, :] = zero8
+
+        for ref in (fine.at[g, 0], fine.at[g, 1], final.at[g]):
+            for y in (0, height + 1, height + 2):
+                ref[pl.ds(y * pitch, 8), :] = zero8
+        for y in (-1, height):
+            final[g, pl.ds(at(y), width), :] = jnp.zeros((width, LANES), jnp.float32)
+
+        @pl.loop(0, h + 2 * PAD)
+        def _(y):
+            here = pl.ds(pl.multiple_of(y * coarse_pitch, 8), coarse_pitch)
+            for ref in (coarse.at[g, 1], coarse_load.at[g], coarse_coef.at[g]):
+                ref[here, :] = jnp.zeros((coarse_pitch, LANES), jnp.float32)
 
     def enter():
         barrier = pltpu.get_barrier_semaphore()
@@ -109,37 +118,45 @@
 
         pl.semaphore_wait(barrier, count)
 
+    def fine_place(g, b, side, arrives):
+        if side >= 2:
+            return (column_in if arrives else column_out).at[g, min(b, 1), side - 2]
+        if b == 2:
+            if arrives:
+                return row_in.at[g, side]
+            return final.at[g, pl.ds(at(0) if side == 0 else at(height - 1), width), :]
+        inner, outer = (0, -1) if side == 0 else (height - 1, height)
+        return fine.at[g, b, pl.ds(at(outer if arrives else inner), width), :]
+
     def fine_copy(g, b, side):
-        if side < 2:
-            source = fine.at[g, b, pl.ds(at(0) if side == 0 else at(height - 1), width), :]
-            target = fine.at[g, b, pl.ds(at(height) if side == 0 else at(-1), width), :]
-        else:
-            source = column_out.at[g, b, side - 2]
-            target = column_in.at[g, b, OPPOSITE[side] - 2]
         return pltpu.make_async_remote_copy(
-            src_ref=source, dst_ref=target,
-            send_sem=fine_send.at[g, b, side], recv_sem=fine_recv.at[g, b, OPPOSITE[side]],
+            src_ref=fine_place(g, b, side, False), dst_ref=fine_place(g, b, OPPOSITE[side], True),
+            send_sem=fine_send.at[g, min(b, 1), side], recv_sem=fine_recv.at[g, min(b, 1), OPPOSITE[side]],
             device_id=neighbour(side), device_id_type=MESH,
         )
 
     def fine_arrival(g, b, side):
-        if side < 2:
-            target = fine.at[g, b, pl.ds(at(-1) if side == 0 else at(height), width), :]
-        else:
-            target = column_in.at[g, b, side - 2]
+        place = fine_place(g, b, side, True)
         return pltpu.make_async_remote_copy(
-            src_ref=target, dst_ref=target,
-            send_sem=fine_send.at[g, b, OPPOSITE[side]], recv_sem=fine_recv.at[g, b, side],
+            src_ref=place, dst_ref=place,
+            send_sem=fine_send.at[g, min(b, 1), OPPOSITE[side]], recv_sem=fine_recv.at[g, min(b, 1), side],
             device_id=neighbour(side), device_id_type=MESH,
         )
 
-    def send_fine(g, b):
-        ref = fine.at[g, b]
+    def values_of(g, b):
+        return final.at[g] if b == 2 else fine.at[g, b]
+
+    def send_rows(g, b):
+        for side in (0, 1):
+            pl.when(has[side])(lambda side=side: fine_copy(g, b, side).start())
+
+    def send_columns(g, b):
+        ref = values_of(g, b)
         for side, x in ((2, 0), (3, width - 1)):
-            out = column_out.at[g, b, side - 2]
+            out = column_out.at[g, min(b, 1), side - 2]
             for i in range(height // 8):
                 out[pl.ds(8 * i, 8), :] = ref[pl.ds(at(8 * i) + x, 8, stride=pitch), :]
-        for side in range(4):
+        for side in (2, 3):
             pl.when(has[side])(lambda side=side: fine_copy(g, b, side).start())
 
     def sent_fine(g, b):
@@ -147,44 +164,56 @@
             pl.when(has[side])(lambda side=side: fine_copy(g, b, side).wait_send())
 
     def receive_fine(g, b):
-        ref = fine.at[g, b]
-        for side in range(4):
+        ref = values_of(g, b)
+        for side in (2, 3, 0, 1):
             pl.when(has[side])(lambda side=side: fine_arrival(g, b, side).wait_recv())
         for side, x in ((2, -1), (3, width)):
 
             @pl.when(has[side])
             def _():
-                column = column_in.at[g, b, side - 2]
+                column = column_in.at[g, min(b, 1), side - 2]
                 for i in range(height // 8):
                     ref[pl.ds(at(8 * i) + x, 8, stride=pitch), :] = column[pl.ds(8 * i, 8), :]
 
-    def fine_loop(g, b, finish, rows=8):
+    rows = 8
+    chunks = height // rows
+
+    def fine_chunk(g, b, i, finish):
         ref = fine.at[g, b]
-
-        @pl.loop(0, height // rows)
+        top = i * rows
+        for p in range(width // part):
+            centre = [
+                ref[pl.ds(pl.multiple_of(at(top + r - 1) + p * part, 8), part), :]
+                for r in range(rows + 2)
+            ]
+            for r in range(rows):
+                here = at(top + r) + p * part
+                around = (centre[r] + centre[r + 2]) + (
+                    ref[pl.ds(here - 1, part), :] + ref[pl.ds(here + 1, part), :]
+                )
+                flat = pl.multiple_of((top + r) * width + p * part, 8)
+                finish(top, r, p, pl.multiple_of(here, 8), flat, centre[r + 1], around)
+
+    def fine_loop(g, b, finish, between):
+        @pl.loop(0, 2)
         def _(i):
-            top = i * rows
-            for p in range(width // part):
-                centre = [
-                    ref[pl.ds(pl.multiple_of(at(top + r - 1) + p * part, 8), part), :]
-                    for r in range(rows + 2)
-                ]
-                for r in range(rows):
-                    here = at(top + r) + p * part
-                    around = (centre[r] + centre[r + 2]) + (
-                        ref[pl.ds(here - 1, part), :] + ref[pl.ds(here + 1, part), :]
-                    )
-                    flat = pl.multiple_of((top + r) * width + p * part, 8)
-                    finish(top, r, p, pl.multiple_of(here, 8), flat, centre[r + 1], around)
-
-    def sweep_fine(g, b):
-        out = fine.at[g, 1 - b]
+            fine_chunk(g, b, i * (chunks - 1), finish)
+
+        between()
+
+        @pl.loop(1, chunks - 1)
+        def _(i):
+            fine_chunk(g, b, i, finish)
+
+    def sweep_fine(g, b, new):
+        out = values_of(g, new)
 
         def finish(top, r, p, here, flat, centre, around):
             total = load[g, pl.ds(flat, part), :] + around
             out[pl.ds(here, part), :] = KEEP * centre + coef[g, pl.ds(flat, part), :] * total
 
-        fine_loop(g, b, finish)
+        fine_loop(g, b, finish, lambda: send_rows(g, new))
+        send_columns(g, new)
 
     def defect(g, flat, centre, around):
         return (load[g, pl.ds(flat, part), :] + around) - (4.0 + mass[g, pl.ds(flat, part), :]) * centre
@@ -195,20 +224,20 @@
         return scratch[pl.ds(0, part // 2, stride=2), :] + scratch[pl.ds(1, part // 2, stride=2), :]
 
     def coarsen_mass(g):
-        rows = 4
-
-        @pl.loop(0, height // rows)
+        step = 4
+
+        @pl.loop(0, height // step)
         def _(i):
             for p in range(width // part):
-                for r in range(0, rows, 2):
+                for r in range(0, step, 2):
                     pair = []
                     for s in range(2):
-                        flat = pl.multiple_of((i * rows + r + s) * width + p * part, 8)
+                        flat = pl.multiple_of((i * step + r + s) * width + p * part, 8)
                         here = mass[g, pl.ds(flat, part), :]
                         coef[g, pl.ds(flat, part), :] = WEIGHT / (4.0 + here)
                         pair.append(here)
-                    summed = 0.5 * halve(temp, p * (rows // 2) + r // 2, pair[0] + pair[1])
-                    place = coarse_at(i * (rows // 2) + r // 2) + p * (part // 2)
+                    summed = 0.5 * halve(temp, p * (step // 2) + r // 2, pair[0] + pair[1])
+                    place = coarse_at(i * (step // 2) + r // 2) + p * (part // 2)
                     coarse_coef[g, pl.ds(pl.multiple_of(place, 8), part // 2), :] = WEIGHT / (4.0 + summed)
 
     def coarsen_defect(g, b):
@@ -223,13 +252,8 @@
                 place = coarse_at(top // 2 + r // 2) + p * (part // 2)
                 coarse_load[g, pl.ds(pl.multiple_of(place, 8), part // 2), :] = summed
 
-        fine_loop(g, b, finish)
-
-    def remain(g, b):
-        def finish(top, r, p, here, flat, centre, around):
-            coef[g, pl.ds(flat, part), :] = defect(g, flat, centre, around)
-
-        fine_loop(g, b, finish)
+        fine_loop(g, b, finish, lambda: send_coarse(g, 1, DEPTHS[0], coarse_load.at[g], (0, 1)))
+        send_coarse(g, 1, DEPTHS[0], coarse_load.at[g], (2, 3, 4, 5, 6, 7))
 
     def blocks(side, depth):
         corner = depth - 1
@@ -289,12 +313,13 @@
             device_id=neighbour(side), device_id_type=MESH,
         )
 
-    def send_coarse(g, e, depth, ref):
-        for side in sides_of(depth):
+    def send_coarse(g, e, depth, ref, sides=(4, 5, 6, 7, 0, 1, 2, 3)):
+        sides = [side for side in sides if side in sides_of(depth)]
+        for side in sides:
             rows, columns, y0, x0, _, _ = blocks(side, depth)
             out = edge_out.at[g, e, side] if side < 4 else corner_out.at[g, e, side - 4]
             move(rows, columns, ref, lambda y: coarse_at(y0 + y) + x0, out, lambda y: y * columns)
-        for side in sides_of(depth):
+        for side in sides:
             pl.when(has[side])(lambda side=side: coarse_copy(g, e, side, depth).start())
 
     def receive_coarse(g, e, depth, ref):
@@ -373,49 +398,38 @@
                     here = pl.ds(at(p * part + 8 * i) + x, 8, stride=pitch)
                     ref[here, :] = ref[here, :] + wide[8 * i : 8 * i + 8]
 
-    def write_solution(g, b):
-        ref = fine.at[g, b]
-
-        @pl.loop(0, height)
-        def _(y):
-            pltpu.make_async_copy(
-                ref.at[pl.ds(pl.multiple_of(at(y), 8), width), :],
-                sol_hbm.at[pl.ds(pl.multiple_of(y * width, 8), width), group_lanes(g)],
-                out_sem.at[0, g],
-            ).start()
-
-    def remaining_copy(g):
-        return pltpu.make_async_copy(coef.at[g], rem_hbm.at[:, group_lanes(g)], out_sem.at[1, g])
-
     both = range(GROUPS)
-    start_inputs()
-    clear()
+    start_values(0)
+    clear_rows()
+    start_values(1)
+    for g in both:
+        start_terms(g)
     enter()
     for g in both:
         wait_input(0, g)
-        send_fine(g, 0)
-    for g in both:
+        send_rows(g, 0)
+        send_columns(g, 0)
+    for g in both:
+        clear_rest(g)
         wait_input(1, g)
         coarsen_mass(g)
         wait_input(2, g)
+    parts = ((0, 1), (2, 4, 5), (3, 6, 7))
     now = 0
     for sweep in range(BEFORE):
         for g in both:
             receive_fine(g, now)
             if sweep >= 1:
                 sent_fine(g, 1 - now)
-            sweep_fine(g, now)
-            send_fine(g, 1 - now)
-            if sweep < GROUPS:
-                send_coarse(sweep, 0, DEPTHS[0], coarse_coef.at[sweep]) if g == GROUPS - 1 else None
+            sweep_fine(g, now, 1 - now)
+            send_coarse(g, 0, DEPTHS[0], coarse_coef.at[g], parts[sweep])
         now = 1 - now
     for g in both:
         receive_fine(g, now)
         coarsen_defect(g, now)
-        send_coarse(g, 1, DEPTHS[0], coarse_load.at[g])
     for g in both:
         receive_coarse(g, 0, DEPTHS[0], coarse_coef.at[g])
-    inner, valid, c = 1, DEPTHS[0], 0
+    inner, c = 1, 0
     for e, depth in enumerate(DEPTHS):
         last = e == len(DEPTHS) - 1
         count = depth - 1 if last else depth
@@ -435,29 +449,75 @@
                 sent_fine(g, now)
                 correct(g, now, b)
                 sent_fine(g, 1 - now)
-                sweep_fine(g, now)
-                send_fine(g, 1 - now)
+                sweep_fine(g, now, 1 - now)
         c = (c + count) % 2
         inner += count
-    assert inner == INNER
-    now = 1 - now
-    for g in both:
-        receive_fine(g, now)
-        sweep_fine(g, now)
-        send_fine(g, 1 - now)
-        write_solution(g, 1 - now)
-    now = 1 - now
-    for g in both:
-        receive_fine(g, now)
-        remain(g, now)
-        remaining_copy(g).start()
-    for g in both:
-        for b in range(2):
-            sent_fine(g, b)
+    assert inner == INNER and now == 1
+    for g in both:
+        receive_fine(g, 0)
+        sweep_fine(g, 0, 2)
         for e in range(len(DEPTHS) + 1):
             sent_coarse(g, e, DEPTHS[max(e - 1, 0)])
-        pltpu.make_async_copy(coef.at[g], sol_hbm.at[:, group_lanes(g)], out_sem.at[0, g]).wait()
-        remaining_copy(g).wait()
+    for g in both:
+        receive_fine(g, 2)
+        for side, y in ((0, -1), (1, height)):
+
+            @pl.when(has[side])
+            def _():
+                final[g, pl.ds(at(y), width), :] = row_in[g, side]
+
+        sent_fine(g, 0)
+        sent_fine(g, 2)
+
+
+def finish_kernel(height, width, final, load, mass, sol_hbm, rem_hbm, rem, sol_sem, rem_sem):
+    pitch, part, rows = width + 8, min(32, width), 8
+    chunks = 2 if height % (2 * rows) == 0 else 1
+    span = height // chunks
+
+    def group_lanes(g):
+        return pl.ds(g * LANES, LANES)
+
+    def at(y):
+        return (y + 1) * pitch + 8
+
+    def remaining_copy(g, c):
+        here = pl.ds(c * span * width, span * width)
+        return pltpu.make_async_copy(rem.at[g, here, :], rem_hbm.at[here, group_lanes(g)], rem_sem.at[g, c])
+
+    for g in range(GROUPS):
+
+        @pl.loop(0, height)
+        def _(y):
+            pltpu.make_async_copy(
+                final.at[g, pl.ds(pl.multiple_of(at(y), 8), width), :],
+                sol_hbm.at[pl.ds(pl.multiple_of(y * width, 8), width), group_lanes(g)],
+                sol_sem.at[g],
+            ).start()
+
+        for c in range(chunks):
+
+            @pl.loop(0, span // rows)
+            def _(i):
+                top = c * span + i * rows
+                for p in range(width // part):
+                    centre = [
+                        final[g, pl.ds(pl.multiple_of(at(top + r - 1) + p * part, 8), part), :]
+                        for r in range(rows + 2)
+                    ]
+                    for r in range(rows):
+                        here = at(top + r) + p * part
+                        around = (centre[r] + centre[r + 2]) + (
+                            final[g, pl.ds(here - 1, part), :] + final[g, pl.ds(here + 1, part), :]
+                        )
+                        flat = pl.ds(pl.multiple_of((top + r) * width + p * part, 8), part)
+                        rem[g, flat, :] = (load[g, flat, :] + around) - (4.0 + mass[g, flat, :]) * centre[r + 1]
+
+            remaining_copy(g, c).start()
+    for g in range(GROUPS):
+        for c in range(chunks):
+            remaining_copy(g, c).wait()
+        pltpu.make_async_copy(rem.at[g], sol_hbm.at[:, group_lanes(g)], sol_sem.at[g]).wait()
 
 
 def body(load_terms, start_values, reaction_rate):
@@ -471,16 +531,21 @@
     corner = -(-((max(DEPTHS) - 1) ** 2) // 8) * 8
     f32 = jnp.float32
     any_space = pl.BlockSpec(memory_space=pl.ANY)
-    results = pl.pallas_call(
+    vmem_space = pl.BlockSpec(memory_space=pltpu.VMEM)
+    cells = height * width
+    held = pl.pallas_call(
         functools.partial(kernel, height, width),
-        out_shape=[jax.ShapeDtypeStruct(flat, f32)] * 2,
+        out_shape=[
+            pltpu.VMEM((GROUPS, fine_rows, LANES), f32),
+            pltpu.VMEM((GROUPS, cells, LANES), f32),
+            pltpu.VMEM((GROUPS, cells, LANES), f32),
+        ],
         in_specs=[any_space] * 3,
-        out_specs=[any_space] * 2,
+        out_specs=[vmem_space] * 3,
         scratch_shapes=[
             pltpu.VMEM((GROUPS, 2, fine_rows, LANES), f32),
-            pltpu.VMEM((GROUPS, height * width, LANES), f32),
-            pltpu.VMEM((GROUPS, height * width, LANES), f32),
-            pltpu.VMEM((GROUPS, height * width, LANES), f32),
+            pltpu.VMEM((GROUPS, cells, LANES), f32),
+            pltpu.VMEM((GROUPS, 2, width, LANES), f32),
             pltpu.VMEM((GROUPS, 2, 2, height, LANES), f32),
             pltpu.VMEM((GROUPS, 2, 2, height, LANES), f32),
             pltpu.VMEM((GROUPS, 2, coarse_rows, LANES), f32),
@@ -492,16 +557,27 @@
             pltpu.VMEM((GROUPS, exchanges, 4, corner, LANES), f32),
             pltpu.VMEM((8, min(32, width), LANES), f32),
             pltpu.SemaphoreType.DMA((3, GROUPS)),
-            pltpu.SemaphoreType.DMA((2, GROUPS)),
             pltpu.SemaphoreType.DMA((GROUPS, 2, 4)),
             pltpu.SemaphoreType.DMA((GROUPS, 2, 4)),
             pltpu.SemaphoreType.DMA((GROUPS, exchanges, 8)),
             pltpu.SemaphoreType.DMA((GROUPS, exchanges, 8)),
         ],
         compiler_params=pltpu.CompilerParams(
-            collective_id=0, has_side_effects=True, vmem_limit_bytes=50 * 1024 * 1024
+            collective_id=0, has_side_effects=True, vmem_limit_bytes=48 * 1024 * 1024
         ),
     )(load_terms.reshape(flat), start_values.reshape(flat), reaction_rate.reshape(flat))
+    results = pl.pallas_call(
+        functools.partial(finish_kernel, height, width),
+        out_shape=[jax.ShapeDtypeStruct(flat, f32)] * 2,
+        in_specs=[vmem_space] * 3,
+        out_specs=[any_space] * 2,
+        scratch_shapes=[
+            pltpu.VMEM((GROUPS, cells, LANES), f32),
+            pltpu.SemaphoreType.DMA((GROUPS,)),
+            pltpu.SemaphoreType.DMA((GROUPS, 2)),
+        ],
+        compiler_params=pltpu.CompilerParams(vmem_limit_bytes=24 * 1024 * 1024),
+    )(*held)
     return tuple(result.reshape(height, width, layers) for result in results)
 
 

time: 91.9 us -> 79.4 us (0.86); the launches traced: 91.7 us -> 78 us
  Pallas kernels: 84.2 us -> 77.3 us
  local copies, waits for them, and re-layouts: 6.87 us -> 0 us
    unnamed x4 -> x0, local copies, waits for them, and re-layouts: 6.87 us -> none
    pallas_call x1 -> x2, Pallas kernels: 84.2 us -> 77.3 us  [the longest x1 73.6 us: body(): pl.pallas_call(functools.partial(kernel, height, width), out_shape=[pltpu...]
where the time goes in v2:
time: 79.4 us; the launch traced here: 78 us
  Pallas kernels  77.3 us (97%)
    pallas_call x1, Pallas kernels, body(): pl.pallas_call(functools.partial(kernel, height, width), out_shape=[pltpu...  73.6 us
    pallas_call x1, Pallas kernels, body(): pl.pallas_call(functools.partial(finish_kernel, height, width), out_shape...  3.78 us

profile of v2, /device:TPU:57, one launch (start us, length us, event | category | flops | bytes accessed | tf_op | source)
XLA Modules:
  0.0 78.0 jit_solution(12424657421960742612)
XLA Ops:
  0.6 73.6 %shard_map.50 = (f32[2,4760,128]{2,1,0:T(8,128)S(1)}, f32[2,4096,128]{2,1,0:T(8,128)S(1)}, f32[2,4096,128]{2,1,0:T(8,128)S(1)}) custom-call(f32[4096,256]{1,0:T(8,128)} %bitcast.5, f32[4096,256]{1,0:T(8,128)} %bitcast.6, f32[4096,256]{1,0:T(8,128)} %bitcast.7), custom_call_target="tpu_custom_call" | custom-call | tf_op jit(solution)/shard_map/pallas_call | solution.py:536
  74.2 3.8 %shard_map.51 = (f32[4096,256]{1,0:T(8,128)}, f32[4096,256]{1,0:T(8,128)}) custom-call(f32[2,4760,128]{2,1,0:T(8,128)S(1)} %get-tuple-element.7.final, f32[2,4096,128]{2,1,0:T(8,128)S(1)} %get-tuple-element.8.load, f32[2,4096,128]{2,1,0:T(8,128)S(1)} %get-tuple-element.9.mass), custom_call_target="tpu_custom_call" | custom-call | tf_op jit(solution)/shard_map/pallas_call | solution.py:569

commit v3 on v2

--- a/solution.py
+++ b/solution.py
@@ -12,7 +12,8 @@
 INNER = 13
 LANES = 128
 GROUPS = 2
-DEPTHS = (3, 3, 3, 4)
+DEPTHS = (2, 3, 3, 3, 2)
+PARTS = ((), (0, 1), (2, 4, 5), (3, 6, 7))
 PAD = 5
 WEIGHT = np.float32(0.8)
 KEEP = np.float32(1.0) - WEIGHT
@@ -77,10 +78,13 @@
         pltpu.make_async_copy(source.at[:, group_lanes(g)], target.at[g], load_sem.at[which, g]).wait()
 
     def clear_rows():
-        for g in range(GROUPS):
-            for b in range(2):
-                fine[g, b, pl.ds(at(-1), width), :] = jnp.zeros((width, LANES), jnp.float32)
-                fine[g, b, pl.ds(at(height), width), :] = jnp.zeros((width, LANES), jnp.float32)
+        for side, y in ((0, -1), (1, height)):
+
+            @pl.when(jnp.logical_not(has[side]))
+            def _():
+                for g in range(GROUPS):
+                    for b in range(2):
+                        fine[g, b, pl.ds(at(y), width), :] = jnp.zeros((width, LANES), jnp.float32)
 
     def clear_rest(g):
         zero8 = jnp.zeros((8, LANES), jnp.float32)
@@ -106,7 +110,7 @@
             for ref in (coarse.at[g, 1], coarse_load.at[g], coarse_coef.at[g]):
                 ref[here, :] = jnp.zeros((coarse_pitch, LANES), jnp.float32)
 
-    def enter():
+    def greet():
         barrier = pltpu.get_barrier_semaphore()
         count = jnp.int32(0)
         for side in range(8):
@@ -116,7 +120,7 @@
             def _():
                 pl.semaphore_signal(barrier, inc=1, device_id=neighbour(side), device_id_type=MESH)
 
-        pl.semaphore_wait(barrier, count)
+        return barrier, count
 
     def fine_place(g, b, side, arrives):
         if side >= 2:
@@ -294,6 +298,9 @@
             for y in range(rows):
                 target[pl.ds(target_at(y), columns), :] = source[pl.ds(source_at(y), columns), :]
 
+    def slot(e):
+        return 0 if e == 0 else 1 + (e - 1) % 2
+
     def sides_of(depth):
         return range(8 if depth > 1 else 4)
 
@@ -301,7 +308,7 @@
         out, _, there = buffers(g, e, side, depth)
         return pltpu.make_async_remote_copy(
             src_ref=out, dst_ref=there,
-            send_sem=coarse_send.at[g, e, side], recv_sem=coarse_recv.at[g, e, OPPOSITE[side]],
+            send_sem=coarse_send.at[g, slot(e), side], recv_sem=coarse_recv.at[g, slot(e), OPPOSITE[side]],
             device_id=neighbour(side), device_id_type=MESH,
         )
 
@@ -309,7 +316,7 @@
         _, here, _ = buffers(g, e, side, depth)
         return pltpu.make_async_remote_copy(
             src_ref=here, dst_ref=here,
-            send_sem=coarse_send.at[g, e, OPPOSITE[side]], recv_sem=coarse_recv.at[g, e, side],
+            send_sem=coarse_send.at[g, slot(e), OPPOSITE[side]], recv_sem=coarse_recv.at[g, slot(e), side],
             device_id=neighbour(side), device_id_type=MESH,
         )
 
@@ -399,12 +406,13 @@
                     ref[here, :] = ref[here, :] + wide[8 * i : 8 * i + 8]
 
     both = range(GROUPS)
-    start_values(0)
+    barrier, count = greet()
+    for g in both:
+        start_values(g)
+    for g in both:
+        start_terms(g)
     clear_rows()
-    start_values(1)
-    for g in both:
-        start_terms(g)
-    enter()
+    pl.semaphore_wait(barrier, count)
     for g in both:
         wait_input(0, g)
         send_rows(g, 0)
@@ -413,8 +421,8 @@
         clear_rest(g)
         wait_input(1, g)
         coarsen_mass(g)
+        send_coarse(g, 0, DEPTHS[0], coarse_coef.at[g], PARTS[0])
         wait_input(2, g)
-    parts = ((0, 1), (2, 4, 5), (3, 6, 7))
     now = 0
     for sweep in range(BEFORE):
         for g in both:
@@ -422,7 +430,7 @@
             if sweep >= 1:
                 sent_fine(g, 1 - now)
             sweep_fine(g, now, 1 - now)
-            send_coarse(g, 0, DEPTHS[0], coarse_coef.at[g], parts[sweep])
+            send_coarse(g, 0, DEPTHS[0], coarse_coef.at[g], PARTS[1 + sweep])
         now = 1 - now
     for g in both:
         receive_fine(g, now)
@@ -444,6 +452,8 @@
                 sweep_coarse(g, b, depth - 1 - i)
                 b = 1 - b
             if not last:
+                if e >= 1:
+                    sent_coarse(g, e, DEPTHS[e - 1])
                 send_coarse(g, 2 + e, DEPTHS[e + 1], coarse.at[g, b])
             else:
                 sent_fine(g, now)
@@ -456,7 +466,7 @@
     for g in both:
         receive_fine(g, 0)
         sweep_fine(g, 0, 2)
-        for e in range(len(DEPTHS) + 1):
+        for e in (0, len(DEPTHS) - 1, len(DEPTHS)):
             sent_coarse(g, e, DEPTHS[max(e - 1, 0)])
     for g in both:
         receive_fine(g, 2)
@@ -470,7 +480,7 @@
         sent_fine(g, 2)
 
 
-def finish_kernel(height, width, final, load, mass, sol_hbm, rem_hbm, rem, sol_sem, rem_sem):
+def finish_kernel(height, width, final, blocked, load, mass, sol_hbm, rem_hbm, rem, sol_sem, rem_sem):
     pitch, part, rows = width + 8, min(32, width), 8
     chunks = 2 if height % (2 * rows) == 0 else 1
     span = height // chunks
@@ -485,16 +495,13 @@
         here = pl.ds(c * span * width, span * width)
         return pltpu.make_async_copy(rem.at[g, here, :], rem_hbm.at[here, group_lanes(g)], rem_sem.at[g, c])
 
+    def solution_copy(g):
+        own = blocked.at[g, pl.ds(1, height), pl.ds(8, width), :]
+        return pltpu.make_async_copy(own, sol_hbm.at[:, :, group_lanes(g)], sol_sem.at[g])
+
     for g in range(GROUPS):
-
-        @pl.loop(0, height)
-        def _(y):
-            pltpu.make_async_copy(
-                final.at[g, pl.ds(pl.multiple_of(at(y), 8), width), :],
-                sol_hbm.at[pl.ds(pl.multiple_of(y * width, 8), width), group_lanes(g)],
-                sol_sem.at[g],
-            ).start()
-
+        solution_copy(g).start()
+    for g in range(GROUPS):
         for c in range(chunks):
 
             @pl.loop(0, span // rows)
@@ -517,14 +524,14 @@
     for g in range(GROUPS):
         for c in range(chunks):
             remaining_copy(g, c).wait()
-        pltpu.make_async_copy(rem.at[g], sol_hbm.at[:, group_lanes(g)], sol_sem.at[g]).wait()
+        solution_copy(g).wait()
 
 
 def body(load_terms, start_values, reaction_rate):
     height, width, layers = load_terms.shape
     h, w = height // 2, width // 2
     flat = (height * width, layers)
-    fine_rows = (height + 2) * (width + 8) + 8
+    fine_rows = (height + 3) * (width + 8)
     coarse_rows = (h + 2 * PAD) * (w + 16)
     exchanges = len(DEPTHS) + 1
     edge = max(DEPTHS) * max(h, w)
@@ -559,8 +566,8 @@
             pltpu.SemaphoreType.DMA((3, GROUPS)),
             pltpu.SemaphoreType.DMA((GROUPS, 2, 4)),
             pltpu.SemaphoreType.DMA((GROUPS, 2, 4)),
-            pltpu.SemaphoreType.DMA((GROUPS, exchanges, 8)),
-            pltpu.SemaphoreType.DMA((GROUPS, exchanges, 8)),
+            pltpu.SemaphoreType.DMA((GROUPS, 3, 8)),
+            pltpu.SemaphoreType.DMA((GROUPS, 3, 8)),
         ],
         compiler_params=pltpu.CompilerParams(
             collective_id=0, has_side_effects=True, vmem_limit_bytes=48 * 1024 * 1024
@@ -568,8 +575,11 @@
     )(load_terms.reshape(flat), start_values.reshape(flat), reaction_rate.reshape(flat))
     results = pl.pallas_call(
         functools.partial(finish_kernel, height, width),
-        out_shape=[jax.ShapeDtypeStruct(flat, f32)] * 2,
-        in_specs=[vmem_space] * 3,
+        out_shape=[
+            jax.ShapeDtypeStruct((height, width, layers), f32),
+            jax.ShapeDtypeStruct(flat, f32),
+        ],
+        in_specs=[vmem_space] * 4,
         out_specs=[any_space] * 2,
         scratch_shapes=[
             pltpu.VMEM((GROUPS, cells, LANES), f32),
@@ -577,7 +587,7 @@
             pltpu.SemaphoreType.DMA((GROUPS, 2)),
         ],
         compiler_params=pltpu.CompilerParams(vmem_limit_bytes=24 * 1024 * 1024),
-    )(*held)
+    )(held[0], held[0].reshape(GROUPS, height + 3, width + 8, LANES), held[1], held[2])
     return tuple(result.reshape(height, width, layers) for result in results)
 
 

time: 79.4 us -> 76.2 us (0.960)
  Pallas kernels: 77.3 us -> 74.4 us
    pallas_call x1, Pallas kernels: 73.6 us -> 71 us  [body(): pl.pallas_call(functools.partial(kernel, height, width), out_shape=[pltpu...]
where the time goes in v3:
time: 76.2 us; the launch traced here: 75 us
  Pallas kernels  74.4 us (98%)
    pallas_call x1, Pallas kernels, body(): pl.pallas_call(functools.partial(kernel, height, width), out_shape=[pltpu...  71 us
    pallas_call x1, Pallas kernels, body(): pl.pallas_call(functools.partial(finish_kernel, height, width), out_shape...  3.35 us

profile of v3, /device:TPU:57, one launch (start us, length us, event | category | flops | bytes accessed | tf_op | source)
XLA Modules:
  0.0 75.0 jit_solution(14376675398091466000)
XLA Ops:
  0.6 71.0 %shard_map.50 = (f32[2,4824,128]{2,1,0:T(8,128)S(1)}, f32[2,4096,128]{2,1,0:T(8,128)S(1)}, f32[2,4096,128]{2,1,0:T(8,128)S(1)}) custom-call(f32[4096,256]{1,0:T(8,128)} %bitcast.6, f32[4096,256]{1,0:T(8,128)} %bitcast.7, f32[4096,256]{1,0:T(8,128)} %bitcast.8), custom_call_target="tpu_custom_call" | custom-call | tf_op jit(solution)/shard_map/pallas_call | solution.py:543
  71.7 3.4 %shard_map.51 = (f32[64,64,256]{2,1,0:T(8,128)}, f32[4096,256]{1,0:T(8,128)}) custom-call(f32[2,4824,128]{2,1,0:T(8,128)S(1)} %get-tuple-element.7.final, f32[2,67,72,128]{3,2,1,0:T(8,128)S(1)} %bitcast.5, f32[2,4096,128]{2,1,0:T(8,128)S(1)} %get-tuple-element.8.load, f32[2,4096,128]{2,1,0:T(8,128)S(1)} %get-tuple-element.9.mass), custom_call_target="tpu_custom_call" | custom-call | tf_op jit(solution)/shard_map/pallas_call | solution.py:576

commit v4 on v3

--- a/solution.py
+++ b/solution.py
@@ -12,7 +12,7 @@
 INNER = 13
 LANES = 128
 GROUPS = 2
-DEPTHS = (2, 3, 3, 3, 2)
+DEPTHS = (2, 3, 2, 3, 3)
 PARTS = ((), (0, 1), (2, 4, 5), (3, 6, 7))
 PAD = 5
 WEIGHT = np.float32(0.8)
@@ -256,8 +256,8 @@
                 place = coarse_at(top // 2 + r // 2) + p * (part // 2)
                 coarse_load[g, pl.ds(pl.multiple_of(place, 8), part // 2), :] = summed
 
-        fine_loop(g, b, finish, lambda: send_coarse(g, 1, DEPTHS[0], coarse_load.at[g], (0, 1)))
-        send_coarse(g, 1, DEPTHS[0], coarse_load.at[g], (2, 3, 4, 5, 6, 7))
+        fine_loop(g, b, finish, lambda: send_coarse(g, 1, DEPTHS[0], coarse_load.at[g], (4, 5, 6, 7, 0, 1)))
+        send_coarse(g, 1, DEPTHS[0], coarse_load.at[g], (2, 3))
 
     def blocks(side, depth):
         corner = depth - 1
@@ -330,7 +330,7 @@
             pl.when(has[side])(lambda side=side: coarse_copy(g, e, side, depth).start())
 
     def receive_coarse(g, e, depth, ref):
-        for side in sides_of(depth):
+        for side in (2, 3, *range(4, len(sides_of(depth))), 0, 1):
 
             @pl.when(has[side])
             def _():

time: 76.2 us -> 75.6 us (level); the launches traced: 75 us -> 75.5 us
  no operation moved by 1% of the time
where the time goes in v4:
time: 75.6 us; the launch traced here: 75.5 us
  Pallas kernels  74.9 us (99%)
    pallas_call x1, Pallas kernels, body(): pl.pallas_call(functools.partial(kernel, height, width), out_shape=[pltpu...  71.5 us
    pallas_call x1, Pallas kernels, body(): pl.pallas_call(functools.partial(finish_kernel, height, width), out_shape...  3.35 us

profile of v4, /device:TPU:57, one launch (start us, length us, event | category | flops | bytes accessed | tf_op | source)
XLA Modules:
  0.0 75.5 jit_solution(16421053333768716426)
XLA Ops:
  0.6 71.5 %shard_map.50 = (f32[2,4824,128]{2,1,0:T(8,128)S(1)}, f32[2,4096,128]{2,1,0:T(8,128)S(1)}, f32[2,4096,128]{2,1,0:T(8,128)S(1)}) custom-call(f32[4096,256]{1,0:T(8,128)} %bitcast.6, f32[4096,256]{1,0:T(8,128)} %bitcast.7, f32[4096,256]{1,0:T(8,128)} %bitcast.8), custom_call_target="tpu_custom_call" | custom-call | tf_op jit(solution)/shard_map/pallas_call | solution.py:543
  72.1 3.4 %shard_map.51 = (f32[64,64,256]{2,1,0:T(8,128)}, f32[4096,256]{1,0:T(8,128)}) custom-call(f32[2,4824,128]{2,1,0:T(8,128)S(1)} %get-tuple-element.7.final, f32[2,67,72,128]{3,2,1,0:T(8,128)S(1)} %bitcast.5, f32[2,4096,128]{2,1,0:T(8,128)S(1)} %get-tuple-element.8.load, f32[2,4096,128]{2,1,0:T(8,128)S(1)} %get-tuple-element.9.mass), custom_call_target="tpu_custom_call" | custom-call | tf_op jit(solution)/shard_map/pallas_call | solution.py:576

commit v5 on v4

--- a/solution.py
+++ b/solution.py
@@ -534,8 +534,8 @@
     fine_rows = (height + 3) * (width + 8)
     coarse_rows = (h + 2 * PAD) * (w + 16)
     exchanges = len(DEPTHS) + 1
-    edge = max(DEPTHS) * max(h, w)
-    corner = -(-((max(DEPTHS) - 1) ** 2) // 8) * 8
+    edge = max(DEPTHS) * max(h, w) + 8
+    corner = -(-((max(DEPTHS) - 1) ** 2) // 8) * 8 + 8
     f32 = jnp.float32
     any_space = pl.BlockSpec(memory_space=pl.ANY)
     vmem_space = pl.BlockSpec(memory_space=pltpu.VMEM)

time: 75.6 us -> 75.6 us (level)
  no operation moved by 1% of the time
where the time goes in v5:
time: 75.6 us; the launch traced here: 75.5 us
  Pallas kernels  74.9 us (99%)
    pallas_call x1, Pallas kernels, body(): pl.pallas_call(functools.partial(kernel, height, width), out_shape=[pltpu...  71.5 us
    pallas_call x1, Pallas kernels, body(): pl.pallas_call(functools.partial(finish_kernel, height, width), out_shape...  3.35 us

profile of v5, /device:TPU:57, one launch (start us, length us, event | category | flops | bytes accessed | tf_op | source)
XLA Modules:
  0.0 75.5 jit_solution(9022035036469314174)
XLA Ops:
  0.6 71.5 %shard_map.50 = (f32[2,4824,128]{2,1,0:T(8,128)S(1)}, f32[2,4096,128]{2,1,0:T(8,128)S(1)}, f32[2,4096,128]{2,1,0:T(8,128)S(1)}) custom-call(f32[4096,256]{1,0:T(8,128)} %bitcast.6, f32[4096,256]{1,0:T(8,128)} %bitcast.7, f32[4096,256]{1,0:T(8,128)} %bitcast.8), custom_call_target="tpu_custom_call" | custom-call | tf_op jit(solution)/shard_map/pallas_call | solution.py:543
  72.1 3.4 %shard_map.51 = (f32[64,64,256]{2,1,0:T(8,128)}, f32[4096,256]{1,0:T(8,128)}) custom-call(f32[2,4824,128]{2,1,0:T(8,128)S(1)} %get-tuple-element.7.final, f32[2,67,72,128]{3,2,1,0:T(8,128)S(1)} %bitcast.5, f32[2,4096,128]{2,1,0:T(8,128)S(1)} %get-tuple-element.8.load, f32[2,4096,128]{2,1,0:T(8,128)S(1)} %get-tuple-element.9.mass), custom_call_target="tpu_custom_call" | custom-call | tf_op jit(solution)/shard_map/pallas_call | solution.py:576
